TPU v7x, 32 devices: a whole 2x2x4 slice. The times are simulated.
32 devices in a mesh: dp: 4 (over y, x), frame: 8 (over z, core).
Axes of the slice: x: 2, y: 2, z: 4, core: 2. Of those that a mesh axis runs over, the one named last changes fastest.
Arguments:
- frames_in: bfloat16 [4, 8, 64, 1024], P('dp', 'frame'), may hold values from -6 to 6
- bottleneck: bfloat16 [4, 4, 1024], P('dp'), may hold values from -6 to 6
- spatial_entry: bfloat16 [1024, 1536], replicated, may hold values from -2 to 2
- spatial_exit: bfloat16 [1024, 512], replicated, may hold values from -0.25 to 0.25
- temporal_entry: bfloat16 [1024, 1536], replicated, may hold values from -2 to 2
- temporal_exit: bfloat16 [1024, 512], replicated, may hold values from -0.25 to 0.25
- output_grad: bfloat16 [4, 8, 64, 1024], P('dp', 'frame'), may hold values from -6 to 6
- joined_grad: bfloat16 [4, 4, 1024], P('dp'), may hold values from -6 to 6
Outputs:
- frames_delta: bfloat16 [4, 8, 64, 1024], P('dp', 'frame')
- bottleneck_delta: bfloat16 [4, 4, 1024], P('dp')
- spatialin_grad: bfloat16 [1024, 1536], P(('dp', 'frame'))
- spatialout_grad: bfloat16 [1024, 512], P(('dp', 'frame'))
- temporalin_grad: bfloat16 [1024, 1536], P(('dp', 'frame'))
- temporalout_grad: bfloat16 [1024, 512], P(('dp', 'frame'))
All inputs are finite; a program needn't handle non-finite values.
Results may differ from a plain program's by a relative error of at most 0.024.
Values may be sent and summed in bfloat16 or wider, within the bound.
A program may use at most 64 MiB of HBM per device.

v0:
```python
import functools
import math

import jax
import jax.numpy as jnp
from jax import lax
from jax.experimental import pallas as pl
from jax.experimental.pallas import tpu as pltpu
from jax.sharding import PartitionSpec as P

HEADS = 8
EPSILON = 1e-05
MESH = pl.DeviceIdType.MESH
F32 = jnp.float32
BF16 = jnp.bfloat16


def dot(left, right, left_dim=1, right_dim=0):
    return lax.dot_general(
        left, right, (((left_dim,), (right_dim,)), ((), ())), preferred_element_type=F32
    )


def normalize(widened):
    centred = widened - jnp.mean(widened, axis=-1, keepdims=True)
    inverse = lax.rsqrt(jnp.mean(centred * centred, axis=-1, keepdims=True) + EPSILON)
    return centred * inverse, inverse


def head_masks(width, dtype):
    lanes = lax.broadcasted_iota(jnp.int32, (1, width), 1)
    size = width // HEADS
    return [
        jnp.where((lanes >= h * size) & (lanes < (h + 1) * size), 1.0, 0.0).astype(dtype)
        for h in range(HEADS)
    ]


def stack_heads(rows):
    return jnp.concatenate([rows * m for m in head_masks(rows.shape[1], rows.dtype)], axis=0)


def merge_heads(stacked):
    count = stacked.shape[0] // HEADS
    masks = head_masks(stacked.shape[1], stacked.dtype)
    total = stacked[:count] * masks[0]
    for h in range(1, HEADS):
        total = total + stacked[h * count : (h + 1) * count] * masks[h]
    return total


def attend(normed_low, entry_ref, mask):
    mixture = dot(normed_low, entry_ref[...]).astype(BF16)
    width = mixture.shape[1] // 3
    queries, key_rows, values = (mixture[:, i * width : (i + 1) * width] for i in range(3))
    factor = 1.0 / math.sqrt(width // HEADS)
    query_stack = stack_heads(queries)
    scores = dot(query_stack, key_rows, 1, 1) * factor
    scores = jnp.where(mask, scores, -1e30)
    scores = scores - jnp.max(scores, axis=-1, keepdims=True)
    expon = jnp.where(mask, jnp.exp(scores), 0.0)
    weights = expon / jnp.sum(expon, axis=-1, keepdims=True)
    weights_low = weights.astype(BF16)
    attended = merge_heads(dot(weights_low, values)).astype(BF16)
    return attended, (query_stack, key_rows, values, weights, weights_low)


def backward_mixture(cotangent, exit_ref, saved, emit):
    query_stack, key_rows, values, weights, weights_low = saved
    factor = 1.0 / math.sqrt(values.shape[1] // HEADS)
    attended_grad = dot(cotangent, exit_ref[...]).astype(BF16)
    grad_stack = stack_heads(attended_grad)
    values_grad = dot(weights_low, grad_stack, 0, 0).astype(BF16)
    emit(2, values_grad)
    softmax_grad = dot(grad_stack, values, 1, 1)
    centre = jnp.sum(weights * softmax_grad, axis=-1, keepdims=True)
    scores_grad = (weights * (softmax_grad - centre) * factor).astype(BF16)
    keys_grad = dot(scores_grad, query_stack, 0, 0).astype(BF16)
    emit(1, keys_grad)
    queries_grad = merge_heads(dot(scores_grad, key_rows)).astype(BF16)
    emit(0, queries_grad)
    return jnp.concatenate([queries_grad, keys_grad, values_grad], axis=1)


def backward_inputs(mixture_grad, entry_ref, cotangent, normed, inverse):
    normed_grad = dot(mixture_grad, entry_ref[...], 1, 1)
    inner = (
        normed_grad
        - jnp.mean(normed_grad, axis=-1, keepdims=True)
        - normed * jnp.mean(normed_grad * normed, axis=-1, keepdims=True)
    )
    return cotangent + inverse * inner


def kernel(
    frame_groups,
    data_groups,
    grad_factor,
    frames_ref,
    bottle_ref,
    output_grad_ref,
    joined_ref,
    spatial_entry_hbm,
    spatial_exit_hbm,
    temporal_entry_hbm,
    temporal_exit_hbm,
    frames_delta_ref,
    bottle_delta_ref,
    spatialin_ref,
    spatialout_ref,
    temporalin_ref,
    temporalout_ref,
    se_ref,
    so_ref,
    te_ref,
    to_ref,
    tokens,
    cot_ref,
    s_normed,
    t_normed,
    og_recv,
    st_send,
    st_recv,
    sg_send,
    sg_recv,
    bot_send,
    bot_pair,
    bot_sum,
    bot_recv,
    s_nl_send,
    s_nl,
    s_att,
    s_c_send,
    s_c,
    s_mg,
    t_nl_send,
    t_nl,
    t_att,
    t_c_send,
    t_c,
    t_mg,
    part,
    pair_recv,
    row_send,
    row_recv,
    load_sem,
    f_send_sem,
    f_recv_sem,
    d_send_sem,
    d_recv_sem,
    pair_sem,
    r_send_sem,
    r_recv_sem,
):
    frame = lax.axis_index("frame")
    data = lax.axis_index("dp")
    patches, model = frames_ref.shape
    bottles = bottle_ref.shape[0]
    rows = tokens.shape[0]
    group = output_grad_ref.shape[1]

    loads = [
        pltpu.make_async_copy(src, dst, load_sem.at[i])
        for i, (src, dst) in enumerate(
            (
                (spatial_entry_hbm, se_ref),
                (spatial_exit_hbm, so_ref),
                (temporal_entry_hbm, te_ref),
                (temporal_exit_hbm, to_ref),
            )
        )
    ]
    loads[0].start()
    loads[1].start()

    barrier = pltpu.get_barrier_semaphore()
    for k in range(1, frame_groups):
        pl.semaphore_signal(
            barrier,
            inc=1,
            device_id={"frame": lax.rem(frame + k, frame_groups)},
            device_id_type=MESH,
        )
    for k in range(1, data_groups):
        pl.semaphore_signal(
            barrier, inc=1, device_id={"dp": lax.rem(data + k, data_groups)}, device_id_type=MESH
        )
    pl.semaphore_wait(barrier, frame_groups + data_groups - 2)

    pending = []

    def push(src_of, dst, axis, phase):
        count = frame_groups if axis == "frame" else data_groups
        me = frame if axis == "frame" else data
        send, recv = (f_send_sem, f_recv_sem) if axis == "frame" else (d_send_sem, d_recv_sem)
        copies = []
        for k in range(1, count):
            peer = lax.rem(me + k, count)
            copy = pltpu.make_async_remote_copy(
                src_ref=src_of(peer),
                dst_ref=dst.at[me],
                send_sem=send.at[phase, k],
                recv_sem=recv.at[phase, k],
                device_id={axis: peer},
                device_id_type=MESH,
            )
            copy.start()
            copies.append(copy)
        pending.extend(copies)
        return copies

    def arrive(copies):
        for copy in copies:
            copy.wait_recv()

    def exchange(send, dst, axis, phase):
        me = frame if axis == "frame" else data
        copies = push(lambda peer: send.at[peer], dst, axis, phase)
        dst[me] = send[me]
        return copies

    def spread(dst, axis, phase):
        me = frame if axis == "frame" else data
        return push(lambda peer: dst.at[me], dst, axis, phase)

    def put_columns(dst, value):
        width = value.shape[1] // data_groups
        for i in range(data_groups):
            dst[i] = value[:, i * width : (i + 1) * width]

    og_copies = exchange(output_grad_ref, og_recv, "frame", 0)

    tokens[:patches] = frames_ref[...].astype(F32)
    tokens[patches:] = jnp.zeros((rows - patches, model), F32)
    tokens[patches : patches + bottles] = bottle_ref[...].astype(F32)
    normed, s_inverse = normalize(tokens[...])
    s_normed[...] = normed
    s_low = normed.astype(BF16)
    loads[0].wait()
    loads[2].start()
    loads[3].start()
    columns = lax.broadcasted_iota(jnp.int32, (HEADS * rows, rows), 1)
    attended, s_saved = attend(s_low, se_ref, columns < patches + bottles)
    loads[1].wait()
    states = (tokens[:patches] + dot(attended[:patches], so_ref[...], 1, 1)).astype(BF16)
    st_send[...] = states.astype(F32).reshape(frame_groups, group, model).astype(BF16)
    st_copies = exchange(st_send, st_recv, "frame", 1)
    put_columns(s_nl_send, s_low)
    s_att[data] = attended
    s_early = exchange(s_nl_send, s_nl, "dp", 0) + spread(s_att, "dp", 1)

    t_rows = frame_groups * group
    arrive(og_copies)
    t_cot = og_recv[...].astype(F32).reshape(t_rows, model)
    t_cot_low = t_cot.astype(BF16)
    put_columns(t_c_send, t_cot_low)
    t_early = exchange(t_c_send, t_c, "dp", 4)
    arrive(st_copies)
    normed, t_inverse = normalize(st_recv[...].astype(F32).reshape(t_rows, model))
    t_normed[...] = normed
    t_low = normed.astype(BF16)
    loads[2].wait()
    shape = (HEADS * t_rows, t_rows)
    row_patch = lax.broadcasted_iota(jnp.int32, shape, 0) & (group - 1)
    column_patch = lax.broadcasted_iota(jnp.int32, shape, 1) & (group - 1)
    attended, t_saved = attend(t_low, te_ref, row_patch == column_patch)
    t_att[data] = attended
    t_early += spread(t_att, "dp", 3)
    put_columns(t_nl_send, t_low)
    t_nl_copies = exchange(t_nl_send, t_nl, "dp", 2)
    loads[3].wait()
    t_copies = {}

    def keep_temporal(i, value):
        t_mg[i, data] = value
        t_copies[i] = spread(t_mg.at[i], "dp", 5 + i)

    mixture_grad = backward_mixture(t_cot_low, to_ref, t_saved, keep_temporal)
    state_grads = backward_inputs(mixture_grad, te_ref, t_cot, t_normed[...], t_inverse)
    sg_send[...] = state_grads.reshape(frame_groups, group, model).astype(BF16)
    sg_copies = exchange(sg_send, sg_recv, "frame", 2)

    side = lax.rem(frame, 2)
    chip = frame // 2
    chips = frame_groups // 2
    owned = part.shape[3]

    def to_partner(src, dst, slot):
        copy = pltpu.make_async_remote_copy(
            src_ref=src,
            dst_ref=dst,
            send_sem=pair_sem.at[0, slot],
            recv_sem=pair_sem.at[1, slot],
            device_id={"frame": chip * 2 + 1 - side},
            device_id_type=MESH,
        )
        copy.start()
        pending.append(copy)
        return copy

    def to_chips(src_of, dst, slot):
        copies = []
        for k in range(1, chips):
            peer = lax.rem(chip + k, chips)
            copy = pltpu.make_async_remote_copy(
                src_ref=src_of(peer),
                dst_ref=dst,
                send_sem=r_send_sem.at[slot, k],
                recv_sem=r_recv_sem.at[slot, k],
                device_id={"frame": peer * 2 + side},
                device_id_type=MESH,
            )
            copy.start()
            copies.append(copy)
        pending.extend(copies)
        return copies

    def partial(slot, left, right):
        count = left.shape[0] * left.shape[1]
        product = dot(
            left[...].reshape(count, left.shape[2]), right[...].reshape(count, right.shape[2]), 0, 0
        ).astype(BF16)
        for i in range(frame_groups):
            part[slot, i % 2, i // 2] = product[i * owned : (i + 1) * owned]
        return to_partner(part.at[slot, 1 - side], pair_recv.at[slot], slot)

    def pass_on(slot, pair_copy):
        pair_copy.wait_recv()
        row_send[slot] = (part[slot, side].astype(F32) + pair_recv[slot].astype(F32)).astype(BF16)
        row_recv[slot, chip] = row_send[slot, chip]
        return to_chips(
            lambda peer: row_send.at[slot, peer], row_recv.at[slot, chip], slot
        )

    arrive(t_early)
    exit_pair = partial(0, t_c, t_att)

    cot_ref[patches:] = jnp.zeros((rows - patches, model), F32)
    cot_ref[patches : patches + bottles] = (
        (joined_ref[...].astype(F32) / frame_groups).astype(BF16).astype(F32)
    )
    exit_rows = pass_on(0, exit_pair)
    arrive(sg_copies)
    cot_ref[:patches] = sg_recv[...].astype(F32).reshape(patches, model)
    s_cot_low = cot_ref[...].astype(BF16)
    put_columns(s_c_send, s_cot_low)
    s_early += exchange(s_c_send, s_c, "dp", 8)
    s_copies = {}

    def keep_and_send(i, value):
        s_mg[i, data] = value
        s_copies[i] = spread(s_mg.at[i], "dp", 9 + i)

    mixture_grad = backward_mixture(s_cot_low, so_ref, s_saved, keep_and_send)
    tokens_grad = backward_inputs(mixture_grad, se_ref, cot_ref[...], s_normed[...], s_inverse)
    frames_delta_ref[...] = tokens_grad[:patches].astype(BF16)
    bot_send[...] = tokens_grad[patches : patches + bottles]
    last_slot = part.shape[0]
    bot_pair_copy = to_partner(bot_send, bot_pair, last_slot)

    width = s_att.shape[2]
    work = [
        ([], t_c, t_att, temporalout_ref, 0),
        (t_nl_copies + t_copies[2], t_nl, t_mg.at[2], temporalin_ref, 2 * width),
        (t_copies[1], t_nl, t_mg.at[1], temporalin_ref, width),
        (t_copies[0], t_nl, t_mg.at[0], temporalin_ref, 0),
        (s_early, s_c, s_att, spatialout_ref, 0),
        (s_copies[2], s_nl, s_mg.at[2], spatialin_ref, 2 * width),
        (s_copies[1], s_nl, s_mg.at[1], spatialin_ref, width),
        (s_copies[0], s_nl, s_mg.at[0], spatialin_ref, 0),
    ]
    pair_copies, row_copies = {}, {0: exit_rows}
    for slot in range(1, last_slot):
        needed, left, right, _, _ = work[slot]
        arrive(needed)
        pair_copies[slot] = partial(slot, left, right)
        if slot == 1:
            bot_pair_copy.wait_recv()
            bot_sum[...] = bot_send[...] + bot_pair[...]
            bot_recv[chip] = bot_sum[...]
            bot_copies = to_chips(lambda peer: bot_sum, bot_recv.at[chip], last_slot)
        else:
            row_copies[slot - 1] = pass_on(slot - 1, pair_copies[slot - 1])
    row_copies[last_slot - 1] = pass_on(last_slot - 1, pair_copies[last_slot - 1])

    arrive(bot_copies)
    bottle_total = bot_recv[0]
    for i in range(1, chips):
        bottle_total = bottle_total + bot_recv[i]
    bottle_delta_ref[...] = bottle_total.astype(BF16)
    for slot, (_, _, _, out, start) in enumerate(work):
        arrive(row_copies[slot])
        summed = row_recv[slot, 0].astype(F32)
        for i in range(1, chips):
            summed = summed + row_recv[slot, i].astype(F32)
        out[:, start : start + width] = (summed * grad_factor).astype(BF16)
    for copy in pending:
        copy.wait_send()


def hand_over(*refs):
    count = len(refs) // 2
    for source, target in zip(refs[:count], refs[count:]):
        target[...] = source[...]


def per_device(
    frames_in,
    bottleneck,
    spatial_entry,
    spatial_exit,
    temporal_entry,
    temporal_exit,
    output_grad,
    joined_grad,
):
    clip_count, frames_local, patches, model = frames_in.shape
    bottles = bottleneck.shape[1]
    frame_groups = lax.axis_size("frame")
    data_groups = lax.axis_size("dp")
    assert clip_count == 1 and frames_local == 1
    entry_width = spatial_entry.shape[1]
    exit_width = spatial_exit.shape[1]
    group = patches // frame_groups
    assert group & (group - 1) == 0 and frame_groups % 2 == 0
    assert entry_width == 3 * exit_width
    chips = frame_groups // 2
    rows = -(-(patches + bottles) // 16) * 16
    t_rows = patches
    block = model // data_groups
    owned = block // frame_groups
    grad_factor = 1.0 / math.sqrt(patches * data_groups * frame_groups)

    def gather_set(count):
        return [
            pltpu.VMEM((data_groups, count, block), BF16),
            pltpu.VMEM((data_groups, count, block), BF16),
            pltpu.VMEM((data_groups, count, exit_width), BF16),
            pltpu.VMEM((data_groups, count, block), BF16),
            pltpu.VMEM((data_groups, count, block), BF16),
            pltpu.VMEM((3, data_groups, count, exit_width), BF16),
        ]

    moved = pltpu.VMEM((frame_groups, group, model), BF16)
    vmem = pl.BlockSpec(memory_space=pltpu.VMEM)
    hbm = pl.BlockSpec(memory_space=pl.ANY)
    outs = pl.pallas_call(
        functools.partial(kernel, frame_groups, data_groups, grad_factor),
        out_shape=(
            jax.ShapeDtypeStruct((patches, model), BF16),
            jax.ShapeDtypeStruct((bottles, model), BF16),
            jax.ShapeDtypeStruct((owned, entry_width), BF16),
            jax.ShapeDtypeStruct((owned, exit_width), BF16),
            jax.ShapeDtypeStruct((owned, entry_width), BF16),
            jax.ShapeDtypeStruct((owned, exit_width), BF16),
        ),
        in_specs=[vmem] * 4 + [hbm] * 4,
        out_specs=[vmem] * 6,
        scratch_shapes=[
            pltpu.VMEM(spatial_entry.shape, BF16),
            pltpu.VMEM(spatial_exit.shape, BF16),
            pltpu.VMEM(temporal_entry.shape, BF16),
            pltpu.VMEM(temporal_exit.shape, BF16),
            pltpu.VMEM((rows, model), F32),
            pltpu.VMEM((rows, model), F32),
            pltpu.VMEM((rows, model), F32),
            pltpu.VMEM((t_rows, model), F32),
            moved,
            moved,
            moved,
            moved,
            moved,
            *[pltpu.VMEM((bottles, model), F32)] * 3,
            pltpu.VMEM((chips, bottles, model), F32),
            *gather_set(rows),
            *gather_set(t_rows),
            pltpu.VMEM((8, 2, chips, owned, exit_width), BF16),
            *[pltpu.VMEM((8, chips, owned, exit_width), BF16)] * 3,
            pltpu.SemaphoreType.DMA((4,)),
            pltpu.SemaphoreType.DMA((6, frame_groups)),
            pltpu.SemaphoreType.DMA((6, frame_groups)),
            pltpu.SemaphoreType.DMA((12, data_groups)),
            pltpu.SemaphoreType.DMA((12, data_groups)),
            pltpu.SemaphoreType.DMA((2, 9)),
            pltpu.SemaphoreType.DMA((9, chips)),
            pltpu.SemaphoreType.DMA((9, chips)),
        ],
        compiler_params=pltpu.CompilerParams(
            collective_id=0, has_side_effects=True, vmem_limit_bytes=61 * 1024 * 1024
        ),
    )(
        frames_in.reshape(patches, model),
        bottleneck.reshape(bottles, model),
        output_grad.reshape(frame_groups, group, model),
        joined_grad.reshape(bottles, model),
        spatial_entry,
        spatial_exit,
        temporal_entry,
        temporal_exit,
    )
    outs = pl.pallas_call(
        hand_over,
        out_shape=[jax.ShapeDtypeStruct(out.shape, out.dtype) for out in outs],
        in_specs=[vmem] * len(outs),
        out_specs=[vmem] * len(outs),
        compiler_params=pltpu.CompilerParams(vmem_limit_bytes=61 * 1024 * 1024),
    )(*outs)
    return (outs[0].reshape(frames_in.shape), outs[1].reshape(bottleneck.shape), *outs[2:])


def solution(mesh):
    return jax.shard_map(
        per_device,
        mesh=mesh,
        in_specs=(
            P("dp", "frame", None, None),
            P("dp", None, None),
            P(),
            P(),
            P(),
            P(),
            P("dp", "frame", None, None),
            P("dp", None, None),
        ),
        out_specs=(
            P("dp", "frame", None, None),
            P("dp", None, None),
            P(("dp", "frame"), None),
            P(("dp", "frame"), None),
            P(("dp", "frame"), None),
            P(("dp", "frame"), None),
        ),
        check_vma=False,
    )
```

profile of v0, /device:TPU:0, one launch (start us, length us, event | category | flops | bytes accessed | tf_op | source)
XLA Modules:
  0.0 55.3 jit_solution(4819198659581302825)
XLA Ops:
  0.6 52.9 %shard_map.127 = (bf16[64,1024]{1,0:T(8,128)(2,1)}, bf16[4,1024]{1,0:T(4,128)(2,1)}, bf16[32,1536]{1,0:T(8,128)(2,1)}, bf16[32,512]{1,0:T(8,128)(2,1)}, bf16[32,...) custom-call(bf16[64,1024]{1,0:T(8,128)(2,1)} %bitcast.6, bf16[4,1024]{1,0:T(4,128)(2,1)} %bitcast.8, ...), custom_call_target="tpu_custom_call" | custom-call | tf_op jit(solution)/shard_map/pallas_call | solution.py:447
  53.5 1.8 %shard_map.128 = (bf16[64,1024]{1,0:T(8,128)(2,1)}, bf16[4,1024]{1,0:T(4,128)(2,1)}, bf16[32,1536]{1,0:T(8,128)(2,1)}, bf16[32,512]{1,0:T(8,128)(2,1)}, bf16[32,...) custom-call(bf16[64,1024]{1,0:T(8,128)(2,1)} %get-tuple-element.18.refs_0_, bf16[4,1024]{1,0:T(4,128)(2,1)} %get-tuple-element.19.refs_1_, ...), custom_call_target="tpu_custom_call" | custom-call | tf_op jit(solution)/shard_map/pallas_call | solution.py:501
where the time goes:
time: 55.5 us; the launch traced here: 55.3 us
  Pallas kernels  54.7 us (99%)
  between operations  0.64 us (1%)
    pallas_call x1, Pallas kernels, per_device(): pl.pallas_call(functools.partial(kernel, frame_groups, data_groups, grad_...  52.9 us
    pallas_call x1, Pallas kernels, per_device(): pl.pallas_call(hand_over, out_shape=[jax.ShapeDtypeStruct(out.shape, out....  1.79 us

commit v1 on v0

v1 whole, which is shorter than its diff:
```python
import functools
import math

import jax
import jax.numpy as jnp
from jax import lax
from jax.experimental import pallas as pl
from jax.experimental.pallas import tpu as pltpu
from jax.sharding import PartitionSpec as P

HEADS = 8
EPSILON = 1e-05
MESH = pl.DeviceIdType.MESH
F32 = jnp.float32
BF16 = jnp.bfloat16


def dot(left, right, left_dim=1, right_dim=0):
    return lax.dot_general(
        left, right, (((left_dim,), (right_dim,)), ((), ())), preferred_element_type=F32
    )


def normalize(widened):
    centred = widened - jnp.mean(widened, axis=-1, keepdims=True)
    inverse = lax.rsqrt(jnp.mean(centred * centred, axis=-1, keepdims=True) + EPSILON)
    return centred * inverse, inverse


def head_masks(width, dtype):
    lanes = lax.broadcasted_iota(jnp.int32, (1, width), 1)
    size = width // HEADS
    return [
        jnp.where((lanes >= h * size) & (lanes < (h + 1) * size), 1.0, 0.0).astype(dtype)
        for h in range(HEADS)
    ]


def stack_heads(rows):
    return jnp.concatenate([rows * m for m in head_masks(rows.shape[1], rows.dtype)], axis=0)


def merge_heads(stacked):
    count = stacked.shape[0] // HEADS
    masks = head_masks(stacked.shape[1], stacked.dtype)
    total = stacked[:count] * masks[0]
    for h in range(1, HEADS):
        total = total + stacked[h * count : (h + 1) * count] * masks[h]
    return total


def attend(normed_low, entry_ref, mask, between):
    mixture = dot(normed_low, entry_ref[...]).astype(BF16)
    between()
    width = mixture.shape[1] // 3
    queries, key_rows, values = (mixture[:, i * width : (i + 1) * width] for i in range(3))
    factor = 1.0 / math.sqrt(width // HEADS)
    query_stack = stack_heads(queries)
    scores = dot(query_stack, key_rows, 1, 1) * factor
    scores = jnp.where(mask, scores, -1e30)
    scores = scores - jnp.max(scores, axis=-1, keepdims=True)
    expon = jnp.where(mask, jnp.exp(scores), 0.0)
    weights = expon / jnp.sum(expon, axis=-1, keepdims=True)
    weights_low = weights.astype(BF16)
    attended = merge_heads(dot(weights_low, values)).astype(BF16)
    return attended, (query_stack, key_rows, values, weights, weights_low)


def backward_mixture(cotangent, exit_ref, saved, emit):
    query_stack, key_rows, values, weights, weights_low = saved
    factor = 1.0 / math.sqrt(values.shape[1] // HEADS)
    attended_grad = dot(cotangent, exit_ref[...]).astype(BF16)
    grad_stack = stack_heads(attended_grad)
    values_grad = dot(weights_low, grad_stack, 0, 0).astype(BF16)
    emit(2, values_grad)
    softmax_grad = dot(grad_stack, values, 1, 1)
    centre = jnp.sum(weights * softmax_grad, axis=-1, keepdims=True)
    scores_grad = (weights * (softmax_grad - centre) * factor).astype(BF16)
    keys_grad = dot(scores_grad, query_stack, 0, 0).astype(BF16)
    emit(1, keys_grad)
    queries_grad = merge_heads(dot(scores_grad, key_rows)).astype(BF16)
    emit(0, queries_grad)
    return jnp.concatenate([queries_grad, keys_grad, values_grad], axis=1)


def backward_inputs(mixture_grad, entry_ref, cotangent, normed, inverse):
    normed_grad = dot(mixture_grad, entry_ref[...], 1, 1)
    inner = (
        normed_grad
        - jnp.mean(normed_grad, axis=-1, keepdims=True)
        - normed * jnp.mean(normed_grad * normed, axis=-1, keepdims=True)
    )
    return cotangent + inverse * inner


def kernel(
    frame_groups,
    row_groups,
    column_groups,
    grad_factor,
    frames_hbm,
    bottle_hbm,
    output_grad_hbm,
    joined_hbm,
    spatial_entry_hbm,
    spatial_exit_hbm,
    temporal_entry_hbm,
    temporal_exit_hbm,
    frames_delta_hbm,
    bottle_delta_hbm,
    spatialin_hbm,
    spatialout_hbm,
    temporalin_hbm,
    temporalout_hbm,
    frames_ref,
    bottle_ref,
    og_send,
    joined_ref,
    se_ref,
    so_ref,
    te_ref,
    to_ref,
    frames_delta_ref,
    bottle_delta_ref,
    spatialin_ref,
    spatialout_ref,
    temporalin_ref,
    temporalout_ref,
    tokens,
    cot_ref,
    s_normed,
    t_normed,
    og_recv,
    st_send,
    st_recv,
    sg_send,
    sg_recv,
    bot_sum,
    bot_recv,
    s_nl_send,
    s_nl,
    s_att_send,
    s_att,
    s_c_send,
    s_c,
    s_mg_send,
    s_mg,
    t_nl_send,
    t_nl,
    t_att_send,
    t_att,
    t_c_send,
    t_c,
    t_mg_send,
    t_mg,
    *tail,
):
    bits = frame_groups.bit_length() - 1
    part = tail[0]
    received = tail[1 : 1 + bits]
    sums = (part,) + tuple(tail[1 + bits : 1 + 2 * bits])
    (
        load_sem,
        out_sem,
        f_send_sem,
        f_recv_sem,
        d_send_sem,
        d_recv_sem,
        r_send_sem,
        r_recv_sem,
        x_send_sem,
        x_recv_sem,
    ) = tail[1 + 2 * bits :]
    frame = lax.axis_index("frame")
    data = lax.axis_index("dp")
    row_at = data // column_groups
    column_at = lax.rem(data, column_groups)
    data_groups = row_groups * column_groups
    patches, model = frames_ref.shape
    bottles = bottle_ref.shape[0]
    rows = tokens.shape[0]
    sent_rows = s_nl.shape[1]
    group = og_send.shape[1]
    width = to_ref.shape[1]
    block = width // column_groups
    side = [lax.rem(frame // (1 << s), 2) for s in range(bits)]

    loads = {}

    def load(name, src, dst):
        loads[name] = pltpu.make_async_copy(src, dst, load_sem.at[len(loads)])
        loads[name].start()

    load("frames", frames_hbm, frames_ref)
    load("bottle", bottle_hbm, bottle_ref)
    load("se", spatial_entry_hbm, se_ref)
    load("og", output_grad_hbm, og_send)
    load("so", spatial_exit_hbm, so_ref)
    load("te", temporal_entry_hbm, te_ref)
    load("to", temporal_exit_hbm, to_ref)
    load("joined", joined_hbm, joined_ref)

    barrier = pltpu.get_barrier_semaphore()
    for k in range(1, frame_groups):
        pl.semaphore_signal(
            barrier,
            inc=1,
            device_id={"frame": lax.rem(frame + k, frame_groups)},
            device_id_type=MESH,
        )
    for k in range(1, data_groups):
        pl.semaphore_signal(
            barrier, inc=1, device_id={"dp": lax.rem(data + k, data_groups)}, device_id_type=MESH
        )

    pending = []

    def push(src, dst, send_sem, recv_sem, device):
        copy = pltpu.make_async_remote_copy(
            src_ref=src,
            dst_ref=dst,
            send_sem=send_sem,
            recv_sem=recv_sem,
            device_id=device,
            device_id_type=MESH,
        )
        copy.start()
        pending.append(copy)
        return copy

    def arrive(copies):
        for copy in copies:
            copy.wait_recv()

    def across(k):
        peer = frame
        for s in range(bits):
            if k >> s & 1:
                peer = peer + (1 << s) * (1 - 2 * side[s])
        return peer

    def exchange_frames(send, dst, phase):
        copies = []
        for k in reversed(range(1, frame_groups)):
            peer = across(k)
            copies.append(
                push(
                    send.at[peer],
                    dst.at[frame],
                    f_send_sem.at[phase, k],
                    f_recv_sem.at[phase, k],
                    {"frame": peer},
                )
            )
        dst[frame] = send[frame]
        return copies

    def spread(send, dst, by_row, phase):
        copies = []
        for k in reversed(range(1, data_groups)):
            peer_row = lax.rem(row_at + k // column_groups, row_groups)
            peer_column = lax.rem(column_at + k % column_groups, column_groups)
            copies.append(
                push(
                    send.at[peer_row if by_row else peer_column],
                    dst.at[data],
                    d_send_sem.at[phase, k],
                    d_recv_sem.at[phase, k],
                    {"dp": peer_row * column_groups + peer_column},
                )
            )
        dst[data] = send[row_at if by_row else column_at]
        return copies

    def put_blocks(dst, value):
        count, kept, size = dst.shape
        for i in range(count):
            dst[i] = value[:kept, i * size : (i + 1) * size]

    def share_rows(send, dst, value, phase):
        put_blocks(send, value)
        return spread(send, dst, True, phase)

    def share_columns(send, dst, value, phase):
        put_blocks(send, value)
        return spread(send, dst, False, phase)

    og_copies = []

    def enter():
        with jax.named_scope("a02_enter"):
            pl.semaphore_wait(barrier, frame_groups + data_groups - 2)
            loads["og"].wait()
            og_copies.extend(exchange_frames(og_send, og_recv, 0))

    with jax.named_scope("a01_norm"):
        loads["frames"].wait()
        loads["bottle"].wait()
        tokens[:patches] = frames_ref[...].astype(F32)
        tokens[patches:] = jnp.zeros((rows - patches, model), F32)
        tokens[patches : patches + bottles] = bottle_ref[...].astype(F32)
        normed, s_inverse = normalize(tokens[...])
        s_normed[...] = normed
        s_low = normed.astype(BF16)
        loads["se"].wait()
    columns = lax.broadcasted_iota(jnp.int32, (HEADS * rows, rows), 1)
    attended, s_saved = attend(s_low, se_ref, columns < patches + bottles, enter)
    with jax.named_scope("a03_states"):
        loads["so"].wait()
        states = (tokens[:patches] + dot(attended[:patches], so_ref[...], 1, 1)).astype(BF16)
        st_send[...] = states.astype(F32).reshape(frame_groups, group, model).astype(BF16)
        st_copies = exchange_frames(st_send, st_recv, 1)
        s_nl_copies = share_rows(s_nl_send, s_nl, s_low, 0)
        s_att_copies = share_columns(s_att_send, s_att, attended, 1)

    t_rows = frame_groups * group
    with jax.named_scope("a04_waitog"):
        arrive(og_copies)
    t_cot = og_recv[...].astype(F32).reshape(t_rows, model)
    t_cot_low = t_cot.astype(BF16)
    t_c_copies = share_rows(t_c_send, t_c, t_cot_low, 4)
    with jax.named_scope("a05_waitst"):
        arrive(st_copies)
    with jax.named_scope("a06_tempfwd"):
        normed, t_inverse = normalize(st_recv[...].astype(F32).reshape(t_rows, model))
        t_normed[...] = normed
        t_low = normed.astype(BF16)
        loads["te"].wait()
        shape = (HEADS * t_rows, t_rows)
        row_patch = lax.broadcasted_iota(jnp.int32, shape, 0) & (group - 1)
        column_patch = lax.broadcasted_iota(jnp.int32, shape, 1) & (group - 1)
        attended, t_saved = attend(t_low, te_ref, row_patch == column_patch, lambda: None)
        t_att_copies = share_columns(t_att_send, t_att, attended, 3)
        t_nl_copies = share_rows(t_nl_send, t_nl, t_low, 2)
    t_copies = {}

    def keep_temporal(i, value):
        t_copies[i] = share_columns(t_mg_send.at[i], t_mg.at[i], value, 5 + i)

    with jax.named_scope("a07_tempbwd"):
        loads["to"].wait()
        mixture_grad = backward_mixture(t_cot_low, to_ref, t_saved, keep_temporal)
        state_grads = backward_inputs(mixture_grad, te_ref, t_cot, t_normed[...], t_inverse)
        sg_send[...] = state_grads.reshape(frame_groups, group, model).astype(BF16)
        sg_copies = exchange_frames(sg_send, sg_recv, 2)

    owned = part.shape[3]

    def gradient(slot, left, right):
        def product_of(low, high):
            count = (high - low) * data_groups
            pieces = [ref[:, low:high] for ref in (left, right)]
            if (high - low) % 16:
                pieces = [p.astype(F32) for p in pieces]
            pieces = [p.reshape(count, p.shape[2]).astype(BF16) for p in pieces]
            return dot(pieces[0], pieces[1], 0, 0)

        product = product_of(0, patches)
        if left.shape[1] > patches:
            product = product + product_of(patches, left.shape[1])
        for f in range(frame_groups):
            place = sum((f >> s & 1) << (bits - 1 - s) for s in range(bits))
            for c in range(column_groups):
                start = (c * frame_groups + f) * owned
                part[slot, place, c] = product[start : start + owned].astype(BF16)

    def halves(step):
        half = frame_groups >> (step + 1)
        return half, side[step] * half, (1 - side[step]) * half

    def reduce_step(item, step):
        half, _, away = halves(step)
        slots = pl.ds(item["first"], item["count"])
        item["copy"] = push(
            sums[step].at[slots, pl.ds(away, half)],
            received[step].at[slots],
            r_send_sem.at[item["id"], step],
            r_recv_sem.at[item["id"], step],
            {"frame": across(1 << step)},
        )

    def advance(item):
        step = item["step"]
        item["step"] = step + 1
        slots = range(item["first"], item["first"] + item["count"])
        if step == 0:
            with jax.named_scope("g%d_wait" % item["id"]):
                arrive(item["needs"])
            with jax.named_scope("g%d_mm" % item["id"]):
                for slot in slots:
                    gradient(slot, *item["operands"](slot))
                reduce_step(item, 0)
        elif step <= bits:
            with jax.named_scope("g%d_r%d" % (item["id"], step)):
                item["copy"].wait_recv()
                half, kept, _ = halves(step - 1)
                for slot in slots:
                    total = sums[step - 1][slot, pl.ds(kept, half)].astype(F32) + received[
                        step - 1
                    ][slot].astype(F32)
                    if step == bits:
                        total = total * grad_factor
                    sums[step][slot] = total.astype(BF16)
                if step < bits:
                    reduce_step(item, step)
                else:
                    item["final"] = []
                    for slot in slots:
                        hand_columns(item, slot)
        elif step == bits + 1:
            with jax.named_scope("g%d_x" % item["id"]):
                arrive(item["final"])

    def target(slot, column):
        out, start = outputs[slot]
        return out.at[:, pl.ds(pl.multiple_of(start + column * block, block), block)]

    def hand_columns(item, slot):
        done = sums[bits]
        for k in range(1, column_groups):
            peer_column = lax.rem(column_at + k, column_groups)
            item["final"].append(
                push(
                    done.at[slot, 0, peer_column],
                    target(slot, column_at),
                    x_send_sem.at[slot, k],
                    x_recv_sem.at[slot, k],
                    {"dp": row_at * column_groups + peer_column},
                )
            )
        target(slot, column_at)[...] = done[slot, 0, column_at]

    outputs = [(temporalout_ref, 0)]
    outputs += [(temporalin_ref, i * width) for i in (2, 1, 0)]
    outputs += [(spatialout_ref, 0)]
    outputs += [(spatialin_ref, i * width) for i in (2, 1, 0)]

    def item(id, first, count, needs, operands):
        return {
            "id": id,
            "first": first,
            "count": count,
            "needs": needs,
            "operands": operands,
            "step": 0,
        }

    exits = item(0, 0, 1, t_c_copies + t_att_copies, lambda slot: (t_c, t_att))
    entries = item(
        1,
        1,
        3,
        t_nl_copies + t_copies[2] + t_copies[1] + t_copies[0],
        lambda slot: (t_nl, t_mg.at[3 - slot]),
    )
    cot_ref[patches:] = jnp.zeros((rows - patches, model), F32)
    loads["joined"].wait()
    cot_ref[patches : patches + bottles] = (
        (joined_ref[...].astype(F32) / frame_groups).astype(BF16).astype(F32)
    )
    advance(exits)
    with jax.named_scope("a08_waitsg"):
        arrive(sg_copies)
    cot_ref[:patches] = sg_recv[...].astype(F32).reshape(patches, model)
    s_cot_low = cot_ref[...].astype(BF16)
    s_c_copies = share_rows(s_c_send, s_c, s_cot_low, 8)
    s_copies = {}

    def keep_spatial(i, value):
        s_copies[i] = share_columns(s_mg_send.at[i], s_mg.at[i], value, 9 + i)

    with jax.named_scope("a09_spatbwd"):
        mixture_grad = backward_mixture(s_cot_low, so_ref, s_saved, keep_spatial)
        tokens_grad = backward_inputs(mixture_grad, se_ref, cot_ref[...], s_normed[...], s_inverse)
        frames_delta_ref[...] = tokens_grad[:patches].astype(BF16)
        bot_sum[0] = tokens_grad[patches : patches + bottles]

    stores = []

    def store(src, dst):
        copy = pltpu.make_async_copy(src, dst, out_sem.at[len(stores)])
        copy.start()
        stores.append(copy)

    store(frames_delta_ref, frames_delta_hbm)

    def bottle_send(step):
        return push(
            bot_sum.at[step],
            bot_recv.at[step],
            r_send_sem.at[6, step],
            r_recv_sem.at[6, step],
            {"frame": across(1 << step)},
        )

    bottle_copy = bottle_send(0)
    bottle_step = 0
    work = [exits, entries]
    work.append(item(2, 4, 1, s_c_copies + s_nl_copies + s_att_copies, lambda slot: (s_c, s_att)))
    for n, i in enumerate((2, 1, 0)):
        work.append(item(3 + n, 5 + n, 1, s_copies[i], lambda slot: (s_nl, s_mg.at[7 - slot])))
    started = 1
    while any(w["step"] < bits + 2 for w in work):
        if started < len(work):
            advance(work[started])
            started += 1
            active = work[: started - 1]
        else:
            active = work
        for w in active:
            if w["step"] < bits + 2:
                advance(w)
        if bottle_step < bits:
            bottle_copy.wait_recv()
            total = bot_sum[bottle_step] + bot_recv[bottle_step]
            bottle_step += 1
            if bottle_step < bits:
                bot_sum[bottle_step] = total
                bottle_copy = bottle_send(bottle_step)
            else:
                bottle_delta_ref[...] = total.astype(BF16)
                store(bottle_delta_ref, bottle_delta_hbm)
        if work[1]["step"] == bits + 2 and len(stores) == 2:
            store(temporalout_ref, temporalout_hbm)
            store(temporalin_ref, temporalin_hbm)
    with jax.named_scope("z1_store"):
        store(spatialout_ref, spatialout_hbm)
        store(spatialin_ref, spatialin_hbm)
        for copy in pending:
            copy.wait_send()
        for copy in stores:
            copy.wait()


def hand_over(*refs):
    count = len(refs) // 2
    for source, target in zip(refs[:count], refs[count:]):
        target[...] = source[...]


def per_device(
    frames_in,
    bottleneck,
    spatial_entry,
    spatial_exit,
    temporal_entry,
    temporal_exit,
    output_grad,
    joined_grad,
):
    clip_count, frames_local, patches, model = frames_in.shape
    bottles = bottleneck.shape[1]
    frame_groups = lax.axis_size("frame")
    data_groups = lax.axis_size("dp")
    assert clip_count == 1 and frames_local == 1
    entry_width = spatial_entry.shape[1]
    exit_width = spatial_exit.shape[1]
    group = patches // frame_groups
    assert group & (group - 1) == 0
    assert frame_groups & (frame_groups - 1) == 0 and data_groups & (data_groups - 1) == 0
    assert entry_width == 3 * exit_width
    bits = frame_groups.bit_length() - 1
    row_groups = 1 << ((data_groups.bit_length() - 1) // 2)
    column_groups = data_groups // row_groups
    rows = -(-(patches + bottles) // 16) * 16
    sent_rows = -(-(patches + bottles) // 8) * 8
    t_rows = patches
    wide = model // row_groups
    block = exit_width // column_groups
    owned = model // data_groups // frame_groups
    grad_factor = 1.0 / math.sqrt(patches * data_groups * frame_groups)

    def gather_set(count):
        return [
            pltpu.VMEM((row_groups, count, wide), BF16),
            pltpu.VMEM((data_groups, count, wide), BF16),
            pltpu.VMEM((column_groups, count, block), BF16),
            pltpu.VMEM((data_groups, count, block), BF16),
            pltpu.VMEM((row_groups, count, wide), BF16),
            pltpu.VMEM((data_groups, count, wide), BF16),
            pltpu.VMEM((3, column_groups, count, block), BF16),
            pltpu.VMEM((3, data_groups, count, block), BF16),
        ]

    moved = pltpu.VMEM((frame_groups, group, model), BF16)
    hbm = pl.BlockSpec(memory_space=pl.ANY)
    vmem = pl.BlockSpec(memory_space=pltpu.VMEM)
    out_shape = (
        jax.ShapeDtypeStruct((patches, model), BF16),
        jax.ShapeDtypeStruct((bottles, model), BF16),
        jax.ShapeDtypeStruct((owned, entry_width), BF16),
        jax.ShapeDtypeStruct((owned, exit_width), BF16),
        jax.ShapeDtypeStruct((owned, entry_width), BF16),
        jax.ShapeDtypeStruct((owned, exit_width), BF16),
    )
    outs = pl.pallas_call(
        functools.partial(kernel, frame_groups, row_groups, column_groups, grad_factor),
        out_shape=out_shape,
        in_specs=[hbm] * 8,
        out_specs=[hbm] * 6,
        scratch_shapes=[
            pltpu.VMEM((patches, model), BF16),
            pltpu.VMEM((bottles, model), BF16),
            moved,
            pltpu.VMEM((bottles, model), BF16),
            pltpu.VMEM(spatial_entry.shape, BF16),
            pltpu.VMEM(spatial_exit.shape, BF16),
            pltpu.VMEM(temporal_entry.shape, BF16),
            pltpu.VMEM(temporal_exit.shape, BF16),
            *[pltpu.VMEM(out.shape, BF16) for out in out_shape],
            pltpu.VMEM((rows, model), F32),
            pltpu.VMEM((rows, model), F32),
            pltpu.VMEM((rows, model), F32),
            pltpu.VMEM((t_rows, model), F32),
            moved,
            moved,
            moved,
            moved,
            moved,
            pltpu.VMEM((bits, bottles, model), F32),
            pltpu.VMEM((bits, bottles, model), F32),
            *gather_set(sent_rows),
            *gather_set(t_rows),
            pltpu.VMEM((8, frame_groups, column_groups, owned, block), BF16),
            *[
                pltpu.VMEM((8, frame_groups >> s, column_groups, owned, block), BF16)
                for s in range(1, bits + 1)
            ]
            * 2,
            pltpu.SemaphoreType.DMA((8,)),
            pltpu.SemaphoreType.DMA((6,)),
            pltpu.SemaphoreType.DMA((3, frame_groups)),
            pltpu.SemaphoreType.DMA((3, frame_groups)),
            pltpu.SemaphoreType.DMA((12, data_groups)),
            pltpu.SemaphoreType.DMA((12, data_groups)),
            pltpu.SemaphoreType.DMA((7, bits)),
            pltpu.SemaphoreType.DMA((7, bits)),
            pltpu.SemaphoreType.DMA((8, column_groups)),
            pltpu.SemaphoreType.DMA((8, column_groups)),
        ],
        compiler_params=pltpu.CompilerParams(
            collective_id=0, has_side_effects=True, vmem_limit_bytes=61 * 1024 * 1024
        ),
    )(
        frames_in.reshape(patches, model),
        bottleneck.reshape(bottles, model),
        output_grad.reshape(frame_groups, group, model),
        joined_grad.reshape(bottles, model),
        spatial_entry,
        spatial_exit,
        temporal_entry,
        temporal_exit,
    )
    outs = pl.pallas_call(
        hand_over,
        out_shape=[jax.ShapeDtypeStruct(out.shape, out.dtype) for out in outs],
        in_specs=[vmem] * len(outs),
        out_specs=[vmem] * len(outs),
        compiler_params=pltpu.CompilerParams(vmem_limit_bytes=61 * 1024 * 1024),
    )(*outs)
    return (outs[0].reshape(frames_in.shape), outs[1].reshape(bottleneck.shape), *outs[2:])


def solution(mesh):
    return jax.shard_map(
        per_device,
        mesh=mesh,
        in_specs=(
            P("dp", "frame", None, None),
            P("dp", None, None),
            P(),
            P(),
            P(),
            P(),
            P("dp", "frame", None, None),
            P("dp", None, None),
        ),
        out_specs=(
            P("dp", "frame", None, None),
            P("dp", None, None),
            P(("dp", "frame"), None),
            P(("dp", "frame"), None),
            P(("dp", "frame"), None),
            P(("dp", "frame"), None),
        ),
        check_vma=False,
    )
```

time: 55.5 us -> 66.5 us (1.20)
  Pallas kernels: 54.7 us -> 65.7 us
    pallas_call x1, Pallas kernels: 52.9 us -> 63.9 us  [per_device(): pl.pallas_call(functools.partial(kernel, frame_groups, row_groups, column...]
where the time goes in v1:
time: 66.5 us; the launch traced here: 66.3 us
  Pallas kernels  65.7 us (99%)
    pallas_call x1, Pallas kernels, per_device(): pl.pallas_call(functools.partial(kernel, frame_groups, row_groups, column...  63.9 us
    pallas_call x1, Pallas kernels, per_device(): pl.pallas_call(hand_over, out_shape=[jax.ShapeDtypeStruct(out.shape, out....  1.79 us

profile of v1, /device:TPU:0, one launch (start us, length us, event | category | flops | bytes accessed | tf_op | source)
XLA Modules:
  0.0 66.3 jit_solution(9613243197191777266)
XLA Ops:
  0.6 63.9 %shard_map.127 = (bf16[64,1024]{1,0:T(8,128)(2,1)}, bf16[4,1024]{1,0:T(4,128)(2,1)}, bf16[32,1536]{1,0:T(8,128)(2,1)}, bf16[32,512]{1,0:T(8,128)(2,1)}, bf16[32,...) custom-call(bf16[64,1024]{1,0:T(8,128)(2,1)} %bitcast.6, bf16[4,1024]{1,0:T(4,128)(2,1)} %bitcast.8, ...), custom_call_target="tpu_custom_call" | custom-call | tf_op jit(solution)/shard_map/pallas_call | solution.py:596
  64.5 1.8 %shard_map.128 = (bf16[64,1024]{1,0:T(8,128)(2,1)}, bf16[4,1024]{1,0:T(4,128)(2,1)}, bf16[32,1536]{1,0:T(8,128)(2,1)}, bf16[32,512]{1,0:T(8,128)(2,1)}, bf16[32,...) custom-call(bf16[64,1024]{1,0:T(8,128)(2,1)} %get-tuple-element.18.refs_0_, bf16[4,1024]{1,0:T(4,128)(2,1)} %get-tuple-element.19.refs_1_, ...), custom_call_target="tpu_custom_call" | custom-call | tf_op jit(solution)/shard_map/pallas_call | solution.py:654

commit v2 on v1

v2 whole, which is shorter than its diff:
```python
import functools
import math

import jax
import jax.numpy as jnp
from jax import lax
from jax.experimental import pallas as pl
from jax.experimental.pallas import tpu as pltpu
from jax.sharding import PartitionSpec as P

HEADS = 8
EPSILON = 1e-05
MESH = pl.DeviceIdType.MESH
F32 = jnp.float32
BF16 = jnp.bfloat16


def dot(left, right, left_dim=1, right_dim=0):
    return lax.dot_general(
        left, right, (((left_dim,), (right_dim,)), ((), ())), preferred_element_type=F32
    )


def normalize(widened):
    centred = widened - jnp.mean(widened, axis=-1, keepdims=True)
    inverse = lax.rsqrt(jnp.mean(centred * centred, axis=-1, keepdims=True) + EPSILON)
    return centred * inverse, inverse


def head_masks(width, dtype):
    lanes = lax.broadcasted_iota(jnp.int32, (1, width), 1)
    size = width // HEADS
    return [
        jnp.where((lanes >= h * size) & (lanes < (h + 1) * size), 1.0, 0.0).astype(dtype)
        for h in range(HEADS)
    ]


def stack_heads(rows):
    return jnp.concatenate([rows * m for m in head_masks(rows.shape[1], rows.dtype)], axis=0)


def merge_heads(stacked):
    count = stacked.shape[0] // HEADS
    masks = head_masks(stacked.shape[1], stacked.dtype)
    total = stacked[:count] * masks[0]
    for h in range(1, HEADS):
        total = total + stacked[h * count : (h + 1) * count] * masks[h]
    return total


def attend(normed_low, entry_ref, mask):
    mixture = dot(normed_low, entry_ref[...]).astype(BF16)
    width = mixture.shape[1] // 3
    queries, key_rows, values = (mixture[:, i * width : (i + 1) * width] for i in range(3))
    factor = 1.0 / math.sqrt(width // HEADS)
    query_stack = stack_heads(queries)
    scores = dot(query_stack, key_rows, 1, 1) * factor
    scores = jnp.where(mask, scores, -1e30)
    scores = scores - jnp.max(scores, axis=-1, keepdims=True)
    expon = jnp.where(mask, jnp.exp(scores), 0.0)
    weights = expon / jnp.sum(expon, axis=-1, keepdims=True)
    weights_low = weights.astype(BF16)
    attended = merge_heads(dot(weights_low, values)).astype(BF16)
    return attended, (query_stack, key_rows, values, weights, weights_low)


def backward_mixture(cotangent, exit_ref, saved, emit):
    query_stack, key_rows, values, weights, weights_low = saved
    factor = 1.0 / math.sqrt(values.shape[1] // HEADS)
    attended_grad = dot(cotangent, exit_ref[...]).astype(BF16)
    grad_stack = stack_heads(attended_grad)
    values_grad = dot(weights_low, grad_stack, 0, 0).astype(BF16)
    emit(2, values_grad)
    softmax_grad = dot(grad_stack, values, 1, 1)
    centre = jnp.sum(weights * softmax_grad, axis=-1, keepdims=True)
    scores_grad = (weights * (softmax_grad - centre) * factor).astype(BF16)
    keys_grad = dot(scores_grad, query_stack, 0, 0).astype(BF16)
    emit(1, keys_grad)
    queries_grad = merge_heads(dot(scores_grad, key_rows)).astype(BF16)
    emit(0, queries_grad)
    return jnp.concatenate([queries_grad, keys_grad, values_grad], axis=1)


def backward_inputs(mixture_grad, entry_ref, cotangent, normed, inverse):
    normed_grad = dot(mixture_grad, entry_ref[...], 1, 1)
    inner = (
        normed_grad
        - jnp.mean(normed_grad, axis=-1, keepdims=True)
        - normed * jnp.mean(normed_grad * normed, axis=-1, keepdims=True)
    )
    return cotangent + inverse * inner


def kernel(
    frame_groups,
    row_groups,
    column_groups,
    grad_factor,
    frames_hbm,
    bottle_hbm,
    output_grad_hbm,
    joined_hbm,
    spatial_entry_hbm,
    spatial_exit_hbm,
    temporal_entry_hbm,
    temporal_exit_hbm,
    frames_delta_hbm,
    bottle_delta_hbm,
    spatialin_hbm,
    spatialout_hbm,
    temporalin_hbm,
    temporalout_hbm,
    frames_ref,
    bottle_ref,
    og_send,
    joined_ref,
    se_ref,
    so_ref,
    te_ref,
    to_ref,
    frames_delta_ref,
    bottle_delta_ref,
    spatialin_ref,
    spatialout_ref,
    temporalin_ref,
    temporalout_ref,
    tokens,
    cot_ref,
    s_normed,
    t_normed,
    og_recv,
    st_send,
    st_recv,
    sg_send,
    sg_recv,
    bot_sum,
    bot_recv,
    s_nl_send,
    s_nl,
    s_att_send,
    s_att,
    s_c_send,
    s_c,
    s_mg_send,
    s_mg,
    t_nl_send,
    t_nl,
    t_att_send,
    t_att,
    t_c_send,
    t_c,
    t_mg_send,
    t_mg,
    *tail,
):
    bits = frame_groups.bit_length() - 1
    part = tail[0]
    received = tail[1 : 1 + bits]
    sums = (part,) + tuple(tail[1 + bits : 1 + 2 * bits])
    (
        load_sem,
        out_sem,
        f_sem,
        d_sem,
        r_sem,
        rs_sem,
        x_sem,
        b_sem,
    ) = tail[1 + 2 * bits :]
    frame = lax.axis_index("frame")
    data = lax.axis_index("dp")
    row_at = data // column_groups
    column_at = lax.rem(data, column_groups)
    data_groups = row_groups * column_groups
    patches, model = frames_ref.shape
    bottles = bottle_ref.shape[0]
    rows = tokens.shape[0]
    group = og_send.shape[1]
    width = to_ref.shape[1]
    block = width // column_groups
    owned = part.shape[3]
    side = [lax.rem(frame // (1 << s), 2) for s in range(bits)]

    loads = {}

    def load(name, src, dst):
        loads[name] = pltpu.make_async_copy(src, dst, load_sem.at[len(loads)])
        loads[name].start()

    load("frames", frames_hbm, frames_ref)
    load("bottle", bottle_hbm, bottle_ref)
    load("se", spatial_entry_hbm, se_ref)
    load("so", spatial_exit_hbm, so_ref)

    barrier = pltpu.get_barrier_semaphore()
    for k in range(1, frame_groups):
        pl.semaphore_signal(
            barrier,
            inc=1,
            device_id={"frame": lax.rem(frame + k, frame_groups)},
            device_id_type=MESH,
        )
    for k in range(1, data_groups):
        pl.semaphore_signal(
            barrier, inc=1, device_id={"dp": lax.rem(data + k, data_groups)}, device_id_type=MESH
        )

    sent = []

    def push(src, dst, send_sem, recv_sem, device):
        copy = pltpu.make_async_remote_copy(
            src_ref=src,
            dst_ref=dst,
            send_sem=send_sem,
            recv_sem=recv_sem,
            device_id=device,
            device_id_type=MESH,
        )
        copy.start()
        return copy

    def drain(view, sem):
        pltpu.make_async_copy(view, view, sem).wait()

    def across(k):
        peer = frame
        for s in range(bits):
            if k >> s & 1:
                peer = peer + (1 << s) * (1 - 2 * side[s])
        return peer

    def exchange_frames(send, dst, phase):
        for k in reversed(range(1, frame_groups)):
            peer = across(k)
            push(
                send.at[peer],
                dst.at[frame],
                f_sem.at[0, phase],
                f_sem.at[1, phase],
                {"frame": peer},
            )
        dst[frame] = send[frame]
        sent.append((dst.at[pl.ds(0, frame_groups - 1)], f_sem.at[0, phase]))

    def arrive_frames(dst, phase):
        drain(dst.at[pl.ds(0, frame_groups - 1)], f_sem.at[1, phase])

    def clip(row, column):
        return row * column_groups + column

    def row_peers():
        return [lax.rem(row_at + k, row_groups) for k in range(1, row_groups)]

    def column_peers():
        return [lax.rem(column_at + k, column_groups) for k in range(1, column_groups)]

    def put_blocks(dst, value):
        count, kept, size = dst.shape
        for i in range(count):
            dst[i] = value[:kept, i * size : (i + 1) * size]

    def share(send, dst, value, by_row, phase):
        put_blocks(send, value)
        mine = row_at if by_row else column_at
        for peer_row in row_peers():
            push(
                send.at[peer_row if by_row else column_at],
                dst.at[data],
                d_sem.at[0, phase],
                d_sem.at[1 if by_row else 2, phase],
                {"dp": clip(peer_row, column_at)},
            )
        for peer_column in column_peers():
            push(
                send.at[row_at if by_row else peer_column],
                dst.at[data],
                d_sem.at[0, phase],
                d_sem.at[2 if by_row else 1, phase],
                {"dp": clip(row_at, peer_column)},
            )
        dst[data] = send[mine]
        sent.append((dst.at[pl.ds(0, data_groups - 1)], d_sem.at[0, phase]))
        return dst, by_row, phase

    def relay(shared):
        dst, by_row, phase = shared
        first = (row_groups if by_row else column_groups) - 1
        drain(dst.at[pl.ds(0, first)], d_sem.at[1, phase])
        for peer_row in row_peers():
            for peer_column in column_peers():
                source = clip(peer_row, column_at) if by_row else clip(row_at, peer_column)
                target = clip(row_at, peer_column) if by_row else clip(peer_row, column_at)
                push(
                    dst.at[source],
                    dst.at[source],
                    d_sem.at[0, phase],
                    d_sem.at[2, phase],
                    {"dp": target},
                )

    def finish(shared):
        dst, by_row, phase = shared
        first = (row_groups if by_row else column_groups) - 1
        drain(dst.at[pl.ds(0, data_groups - 1 - first)], d_sem.at[2, phase])

    def share_direct(send, dst, value, by_row, phase):
        put_blocks(send, value)
        for k in reversed(range(1, data_groups)):
            peer_row = lax.rem(row_at + k // column_groups, row_groups)
            peer_column = lax.rem(column_at + k % column_groups, column_groups)
            push(
                send.at[peer_row if by_row else peer_column],
                dst.at[data],
                d_sem.at[0, phase],
                d_sem.at[1, phase],
                {"dp": clip(peer_row, peer_column)},
            )
        dst[data] = send[row_at if by_row else column_at]
        sent.append((dst.at[pl.ds(0, data_groups - 1)], d_sem.at[0, phase]))
        return dst, by_row, phase

    def finish_direct(shared):
        dst, _, phase = shared
        drain(dst.at[pl.ds(0, data_groups - 1)], d_sem.at[1, phase])

    def gradient(slot, left, right):
        def product_of(low, high):
            count = (high - low) * data_groups
            pieces = [ref[:, low:high] for ref in (left, right)]
            if (high - low) % 16:
                pieces = [p.astype(F32) for p in pieces]
            pieces = [p.reshape(count, p.shape[2]).astype(BF16) for p in pieces]
            return dot(pieces[0], pieces[1], 0, 0)

        product = product_of(0, patches)
        if left.shape[1] > patches:
            product = product + product_of(patches, left.shape[1])
        for f in range(frame_groups):
            place = sum((f >> s & 1) << (bits - 1 - s) for s in range(bits))
            for c in range(column_groups):
                start = (c * frame_groups + f) * owned
                part[slot, place, c] = product[start : start + owned].astype(BF16)

    def send_half(item, step):
        first, count, index = item
        half = frame_groups >> (step + 1)
        slots = pl.ds(first, count)
        push(
            sums[step].at[slots, pl.ds((1 - side[step]) * half, half)],
            received[step].at[slots],
            rs_sem.at[index],
            r_sem.at[index, step],
            {"frame": across(1 << step)},
        )

    def halve(item, step):
        first, count, index = item
        half = frame_groups >> (step + 1)
        drain(received[step].at[pl.ds(first, count)], r_sem.at[index, step])
        for slot in range(first, first + count):
            kept = sums[step][slot, pl.ds(side[step] * half, half)].astype(F32)
            total = kept + received[step][slot].astype(F32)
            if step == bits - 1:
                total = total * grad_factor
            sums[step + 1][slot] = total.astype(BF16)
        if step < bits - 1:
            send_half(item, step + 1)
            return
        sent.append((part.at[pl.ds(first, count), pl.ds(0, frame_groups - 1)], rs_sem.at[index]))
        done = sums[bits]
        for slot in range(first, first + count):
            for peer_column in column_peers():
                push(
                    done.at[slot, 0, peer_column],
                    result(slot, column_at),
                    x_sem.at[0, slot],
                    x_sem.at[1, slot],
                    {"dp": clip(row_at, peer_column)},
                )
            result(slot, column_at)[...] = done[slot, 0, column_at]
            others = done.at[slot, 0, pl.ds(0, column_groups - 1)]
            sent.append((others, x_sem.at[0, slot]))

    def settle(item):
        first, count, _ = item
        for slot in range(first, first + count):
            drain(sums[bits].at[slot, 0, pl.ds(0, column_groups - 1)], x_sem.at[1, slot])

    outputs = [(temporalout_ref, 0)]
    outputs += [(temporalin_ref, i * width) for i in (2, 1, 0)]
    outputs += [(spatialout_ref, 0)]
    outputs += [(spatialin_ref, i * width) for i in (2, 1, 0)]

    def result(slot, column):
        out, start = outputs[slot]
        return out.at[:, pl.ds(pl.multiple_of(start + column * block, block), block)]

    with jax.named_scope("a01_norm"):
        loads["frames"].wait()
        loads["bottle"].wait()
        tokens[:patches] = frames_ref[...].astype(F32)
        tokens[patches:] = jnp.zeros((rows - patches, model), F32)
        tokens[patches : patches + bottles] = bottle_ref[...].astype(F32)
        normed, s_inverse = normalize(tokens[...])
        s_normed[...] = normed
        s_low = normed.astype(BF16)
        loads["se"].wait()
        load("og", output_grad_hbm, og_send)
        load("te", temporal_entry_hbm, te_ref)
        load("to", temporal_exit_hbm, to_ref)
        load("joined", joined_hbm, joined_ref)
    columns = lax.broadcasted_iota(jnp.int32, (HEADS * rows, rows), 1)
    attended, s_saved = attend(s_low, se_ref, columns < patches + bottles)
    with jax.named_scope("a02_states"):
        loads["so"].wait()
        states = (tokens[:patches] + dot(attended[:patches], so_ref[...], 1, 1)).astype(BF16)
        st_send[...] = states.astype(F32).reshape(frame_groups, group, model).astype(BF16)
    with jax.named_scope("a03_enter"):
        pl.semaphore_wait(barrier, frame_groups + data_groups - 2)
        exchange_frames(st_send, st_recv, 0)
        loads["og"].wait()
        exchange_frames(og_send, og_recv, 1)
        s_nl_shared = share(s_nl_send, s_nl, s_low, True, 0)
        s_att_shared = share(s_att_send, s_att, attended, False, 1)

    t_rows = frame_groups * group
    with jax.named_scope("a05_waitst"):
        arrive_frames(st_recv, 0)
    with jax.named_scope("a06_tempfwd"):
        normed, t_inverse = normalize(st_recv[...].astype(F32).reshape(t_rows, model))
        t_normed[...] = normed
        t_low = normed.astype(BF16)
        relay(s_nl_shared)
        relay(s_att_shared)
        t_nl_shared = share(t_nl_send, t_nl, t_low, True, 2)
        loads["te"].wait()
        shape = (HEADS * t_rows, t_rows)
        row_patch = lax.broadcasted_iota(jnp.int32, shape, 0) & (group - 1)
        column_patch = lax.broadcasted_iota(jnp.int32, shape, 1) & (group - 1)
        attended, t_saved = attend(t_low, te_ref, row_patch == column_patch)
        t_att_shared = share(t_att_send, t_att, attended, False, 3)
    with jax.named_scope("a06_waitog"):
        arrive_frames(og_recv, 1)
    t_cot = og_recv[...].astype(F32).reshape(t_rows, model)
    t_cot_low = t_cot.astype(BF16)
    t_c_shared = share(t_c_send, t_c, t_cot_low, True, 4)
    t_shared = {}

    def keep_temporal(i, value):
        t_shared[i] = share(t_mg_send.at[i], t_mg.at[i], value, False, 5 + i)

    with jax.named_scope("a07_tempbwd"):
        loads["to"].wait()
        mixture_grad = backward_mixture(t_cot_low, to_ref, t_saved, keep_temporal)
        state_grads = backward_inputs(mixture_grad, te_ref, t_cot, t_normed[...], t_inverse)
        sg_send[...] = state_grads.reshape(frame_groups, group, model).astype(BF16)
        exchange_frames(sg_send, sg_recv, 2)

    with jax.named_scope("a08_relays"):
        relay(t_nl_shared)
        relay(t_att_shared)
        relay(t_c_shared)
        cot_ref[patches:] = jnp.zeros((rows - patches, model), F32)
        loads["joined"].wait()
        cot_ref[patches : patches + bottles] = (
            (joined_ref[...].astype(F32) / frame_groups).astype(BF16).astype(F32)
        )
        for i in (2, 1, 0):
            relay(t_shared[i])
    temporal_exit_item, temporal_item = (0, 1, 0), (1, 3, 1)
    with jax.named_scope("a09_waitsg"):
        arrive_frames(sg_recv, 2)
    cot_ref[:patches] = sg_recv[...].astype(F32).reshape(patches, model)
    s_cot_low = cot_ref[...].astype(BF16)
    s_c_shared = share_direct(s_c_send, s_c, s_cot_low, True, 8)
    s_shared = {}

    def keep_spatial(i, value):
        s_shared[i] = share_direct(s_mg_send.at[i], s_mg.at[i], value, False, 9 + i)
        if i == 2:
            with jax.named_scope("b1_w"):
                finish(t_att_shared)
                finish(t_c_shared)
            with jax.named_scope("b1_exit"):
                gradient(0, t_c, t_att)
                send_half(temporal_exit_item, 0)
        if i == 1:
            halve(temporal_exit_item, 0)
        if i == 0:
            with jax.named_scope("b2_w"):
                finish(t_nl_shared)
                for n in (2, 1, 0):
                    finish(t_shared[n])
            with jax.named_scope("b2_entry"):
                for slot in (1, 2, 3):
                    gradient(slot, t_nl, t_mg.at[3 - slot])
                send_half(temporal_item, 0)

    with jax.named_scope("b0_spatbwd"):
        mixture_grad = backward_mixture(s_cot_low, so_ref, s_saved, keep_spatial)
        halve(temporal_item, 0)
        tokens_grad = backward_inputs(mixture_grad, se_ref, cot_ref[...], s_normed[...], s_inverse)
        frames_delta_ref[...] = tokens_grad[:patches].astype(BF16)
        bot_sum[0] = tokens_grad[patches : patches + bottles]

    stores = []

    def store(src, dst):
        copy = pltpu.make_async_copy(src, dst, out_sem.at[len(stores)])
        copy.start()
        stores.append(copy)

    store(frames_delta_ref, frames_delta_hbm)

    bottle_copies = []

    def send_bottles(step):
        bottle_copies.append(
            push(
                bot_sum.at[step],
                bot_recv.at[step],
                b_sem.at[0, step],
                b_sem.at[1, step],
                {"frame": across(1 << step)},
            )
        )

    def add_bottles(step):
        bottle_copies[step].wait_recv()
        total = bot_sum[step] + bot_recv[step]
        if step < bits - 1:
            bot_sum[step + 1] = total
            send_bottles(step + 1)
        else:
            bottle_delta_ref[...] = total.astype(BF16)
            store(bottle_delta_ref, bottle_delta_hbm)

    send_bottles(0)
    spatial_a, spatial_b, spatial_c = (4, 2, 2), (6, 1, 3), (7, 1, 4)
    finish(s_nl_shared)
    finish(s_att_shared)
    with jax.named_scope("c1_w"):
        finish_direct(s_c_shared)
        finish_direct(s_shared[2])
    with jax.named_scope("c1_mm"):
        gradient(4, s_c, s_att)
        gradient(5, s_nl, s_mg.at[2])
        send_half(spatial_a, 0)
    with jax.named_scope("c3_w"):
        finish_direct(s_shared[1])
    with jax.named_scope("c3_mm"):
        gradient(6, s_nl, s_mg.at[1])
        send_half(spatial_b, 0)
        halve(spatial_a, 0)
    with jax.named_scope("c4_w"):
        finish_direct(s_shared[0])
    with jax.named_scope("c4_mm"):
        gradient(7, s_nl, s_mg.at[0])
        send_half(spatial_c, 0)
        halve(spatial_b, 0)
    with jax.named_scope("c5_halve"):
        halve(temporal_exit_item, 1)
        halve(spatial_c, 0)
    for step in range(1, bits + 1):
        with jax.named_scope("d%d_t" % step):
            if step > 1 and step < bits:
                halve(temporal_exit_item, step)
            if step < bits:
                halve(temporal_item, step)
        if step < bits:
            with jax.named_scope("d%d_a" % step):
                add_bottles(step - 1)
                halve(spatial_a, step)
            with jax.named_scope("d%d_b" % step):
                halve(spatial_b, step)
            with jax.named_scope("d%d_c" % step):
                halve(spatial_c, step)
    add_bottles(bits - 1)
    with jax.named_scope("e1_settle"):
        settle(temporal_exit_item)
        store(temporalout_ref, temporalout_hbm)
        settle(temporal_item)
        store(temporalin_ref, temporalin_hbm)
        settle(spatial_a)
        store(spatialout_ref, spatialout_hbm)
        settle(spatial_b)
        settle(spatial_c)
        store(spatialin_ref, spatialin_hbm)
    with jax.named_scope("e2_drain"):
        for view, sem in sent:
            drain(view, sem)
        for copy in bottle_copies:
            copy.wait_send()
        for copy in stores:
            copy.wait()


def hand_over(*refs):
    count = len(refs) // 2
    for source, target in zip(refs[:count], refs[count:]):
        target[...] = source[...]


def per_device(
    frames_in,
    bottleneck,
    spatial_entry,
    spatial_exit,
    temporal_entry,
    temporal_exit,
    output_grad,
    joined_grad,
):
    clip_count, frames_local, patches, model = frames_in.shape
    bottles = bottleneck.shape[1]
    frame_groups = lax.axis_size("frame")
    data_groups = lax.axis_size("dp")
    assert clip_count == 1 and frames_local == 1
    entry_width = spatial_entry.shape[1]
    exit_width = spatial_exit.shape[1]
    group = patches // frame_groups
    assert group & (group - 1) == 0
    assert frame_groups & (frame_groups - 1) == 0 and data_groups & (data_groups - 1) == 0
    assert entry_width == 3 * exit_width
    bits = frame_groups.bit_length() - 1
    row_groups = 1 << ((data_groups.bit_length() - 1) // 2)
    column_groups = data_groups // row_groups
    rows = -(-(patches + bottles) // 16) * 16
    sent_rows = -(-(patches + bottles) // 8) * 8
    t_rows = patches
    wide = model // row_groups
    block = exit_width // column_groups
    owned = model // data_groups // frame_groups
    grad_factor = 1.0 / math.sqrt(patches * data_groups * frame_groups)

    def gather_set(count):
        return [
            pltpu.VMEM((row_groups, count, wide), BF16),
            pltpu.VMEM((data_groups, count, wide), BF16),
            pltpu.VMEM((column_groups, count, block), BF16),
            pltpu.VMEM((data_groups, count, block), BF16),
            pltpu.VMEM((row_groups, count, wide), BF16),
            pltpu.VMEM((data_groups, count, wide), BF16),
            pltpu.VMEM((3, column_groups, count, block), BF16),
            pltpu.VMEM((3, data_groups, count, block), BF16),
        ]

    moved = pltpu.VMEM((frame_groups, group, model), BF16)
    hbm = pl.BlockSpec(memory_space=pl.ANY)
    vmem = pl.BlockSpec(memory_space=pltpu.VMEM)
    out_shape = (
        jax.ShapeDtypeStruct((patches, model), BF16),
        jax.ShapeDtypeStruct((bottles, model), BF16),
        jax.ShapeDtypeStruct((owned, entry_width), BF16),
        jax.ShapeDtypeStruct((owned, exit_width), BF16),
        jax.ShapeDtypeStruct((owned, entry_width), BF16),
        jax.ShapeDtypeStruct((owned, exit_width), BF16),
    )
    outs = pl.pallas_call(
        functools.partial(kernel, frame_groups, row_groups, column_groups, grad_factor),
        out_shape=out_shape,
        in_specs=[hbm] * 8,
        out_specs=[hbm] * 6,
        scratch_shapes=[
            pltpu.VMEM((patches, model), BF16),
            pltpu.VMEM((bottles, model), BF16),
            moved,
            pltpu.VMEM((bottles, model), BF16),
            pltpu.VMEM(spatial_entry.shape, BF16),
            pltpu.VMEM(spatial_exit.shape, BF16),
            pltpu.VMEM(temporal_entry.shape, BF16),
            pltpu.VMEM(temporal_exit.shape, BF16),
            *[pltpu.VMEM(out.shape, BF16) for out in out_shape],
            pltpu.VMEM((rows, model), F32),
            pltpu.VMEM((rows, model), F32),
            pltpu.VMEM((rows, model), F32),
            pltpu.VMEM((t_rows, model), F32),
            moved,
            moved,
            moved,
            moved,
            moved,
            pltpu.VMEM((bits, bottles, model), F32),
            pltpu.VMEM((bits, bottles, model), F32),
            *gather_set(sent_rows),
            *gather_set(t_rows),
            pltpu.VMEM((8, frame_groups, column_groups, owned, block), BF16),
            *[
                pltpu.VMEM((8, frame_groups >> s, column_groups, owned, block), BF16)
                for s in range(1, bits + 1)
            ]
            * 2,
            pltpu.SemaphoreType.DMA((8,)),
            pltpu.SemaphoreType.DMA((6,)),
            pltpu.SemaphoreType.DMA((2, 3)),
            pltpu.SemaphoreType.DMA((3, 12)),
            pltpu.SemaphoreType.DMA((5, bits)),
            pltpu.SemaphoreType.DMA((5,)),
            pltpu.SemaphoreType.DMA((2, 8)),
            pltpu.SemaphoreType.DMA((2, bits)),
        ],
        compiler_params=pltpu.CompilerParams(
            collective_id=0, has_side_effects=True, vmem_limit_bytes=61 * 1024 * 1024
        ),
    )(
        frames_in.reshape(patches, model),
        bottleneck.reshape(bottles, model),
        output_grad.reshape(frame_groups, group, model),
        joined_grad.reshape(bottles, model),
        spatial_entry,
        spatial_exit,
        temporal_entry,
        temporal_exit,
    )
    outs = pl.pallas_call(
        hand_over,
        out_shape=[jax.ShapeDtypeStruct(out.shape, out.dtype) for out in outs],
        in_specs=[vmem] * len(outs),
        out_specs=[vmem] * len(outs),
        compiler_params=pltpu.CompilerParams(vmem_limit_bytes=61 * 1024 * 1024),
    )(*outs)
    return (outs[0].reshape(frames_in.shape), outs[1].reshape(bottleneck.shape), *outs[2:])


def solution(mesh):
    return jax.shard_map(
        per_device,
        mesh=mesh,
        in_specs=(
            P("dp", "frame", None, None),
            P("dp", None, None),
            P(),
            P(),
            P(),
            P(),
            P("dp", "frame", None, None),
            P("dp", None, None),
        ),
        out_specs=(
            P("dp", "frame", None, None),
            P("dp", None, None),
            P(("dp", "frame"), None),
            P(("dp", "frame"), None),
            P(("dp", "frame"), None),
            P(("dp", "frame"), None),
        ),
        check_vma=False,
    )
```

time: 66.5 us -> 56.7 us (0.85)
  Pallas kernels: 65.7 us -> 55.9 us
    pallas_call x1, Pallas kernels: 63.9 us -> 54.1 us  [per_device(): pl.pallas_call(functools.partial(kernel, frame_groups, row_groups, column...]
where the time goes in v2:
time: 56.7 us; the launch traced here: 56.6 us
  Pallas kernels  55.9 us (99%)
  between operations  0.64 us (1%)
    pallas_call x1, Pallas kernels, per_device(): pl.pallas_call(functools.partial(kernel, frame_groups, row_groups, column...  54.1 us
    pallas_call x1, Pallas kernels, per_device(): pl.pallas_call(hand_over, out_shape=[jax.ShapeDtypeStruct(out.shape, out....  1.79 us

profile of v2, /device:TPU:0, one launch (start us, length us, event | category | flops | bytes accessed | tf_op | source)
XLA Modules:
  0.0 56.6 jit_solution(12509853377001574766)
XLA Ops:
  0.6 54.1 %shard_map.127 = (bf16[64,1024]{1,0:T(8,128)(2,1)}, bf16[4,1024]{1,0:T(4,128)(2,1)}, bf16[32,1536]{1,0:T(8,128)(2,1)}, bf16[32,512]{1,0:T(8,128)(2,1)}, bf16[32,...) custom-call(bf16[64,1024]{1,0:T(8,128)(2,1)} %bitcast.6, bf16[4,1024]{1,0:T(4,128)(2,1)} %bitcast.8, ...), custom_call_target="tpu_custom_call" | custom-call | tf_op jit(solution)/shard_map/pallas_call | solution.py:660
  54.8 1.8 %shard_map.128 = (bf16[64,1024]{1,0:T(8,128)(2,1)}, bf16[4,1024]{1,0:T(4,128)(2,1)}, bf16[32,1536]{1,0:T(8,128)(2,1)}, bf16[32,512]{1,0:T(8,128)(2,1)}, bf16[32,...) custom-call(bf16[64,1024]{1,0:T(8,128)(2,1)} %get-tuple-element.18.refs_0_, bf16[4,1024]{1,0:T(4,128)(2,1)} %get-tuple-element.19.refs_1_, ...), custom_call_target="tpu_custom_call" | custom-call | tf_op jit(solution)/shard_map/pallas_call | solution.py:716

commit v3 on v2

--- a/solution.py
+++ b/solution.py
@@ -49,10 +49,13 @@
     return total
 
 
-def attend(normed_low, entry_ref, mask):
-    mixture = dot(normed_low, entry_ref[...]).astype(BF16)
-    width = mixture.shape[1] // 3
-    queries, key_rows, values = (mixture[:, i * width : (i + 1) * width] for i in range(3))
+def attend(normed_low, entry_ref, mask, ready=lambda i: None):
+    width = entry_ref.shape[1] // 3
+    parts = []
+    for i in range(3):
+        ready(i)
+        parts.append(dot(normed_low, entry_ref[:, i * width : (i + 1) * width]).astype(BF16))
+    queries, key_rows, values = parts
     factor = 1.0 / math.sqrt(width // HEADS)
     query_stack = stack_heads(queries)
     scores = dot(query_stack, key_rows, 1, 1) * factor
@@ -82,8 +85,8 @@
     return jnp.concatenate([queries_grad, keys_grad, values_grad], axis=1)
 
 
-def backward_inputs(mixture_grad, entry_ref, cotangent, normed, inverse):
-    normed_grad = dot(mixture_grad, entry_ref[...], 1, 1)
+def backward_inputs(mixture_grad, turned_ref, cotangent, normed, inverse):
+    normed_grad = dot(mixture_grad, turned_ref[...])
     inner = (
         normed_grad
         - jnp.mean(normed_grad, axis=-1, keepdims=True)
@@ -119,6 +122,8 @@
     so_ref,
     te_ref,
     to_ref,
+    turned_se,
+    turned_te,
     frames_delta_ref,
     bottle_delta_ref,
     spatialin_ref,
@@ -155,9 +160,9 @@
     *tail,
 ):
     bits = frame_groups.bit_length() - 1
-    part = tail[0]
-    received = tail[1 : 1 + bits]
-    sums = (part,) + tuple(tail[1 + bits : 1 + 2 * bits])
+    part, final = tail[:2]
+    received = tail[2 : 1 + bits]
+    sums = (part,) + tuple(tail[1 + bits : 2 * bits])
     (
         load_sem,
         out_sem,
@@ -167,7 +172,7 @@
         rs_sem,
         x_sem,
         b_sem,
-    ) = tail[1 + 2 * bits :]
+    ) = tail[2 * bits :]
     frame = lax.axis_index("frame")
     data = lax.axis_index("dp")
     row_at = data // column_groups
@@ -190,8 +195,9 @@
 
     load("frames", frames_hbm, frames_ref)
     load("bottle", bottle_hbm, bottle_ref)
-    load("se", spatial_entry_hbm, se_ref)
-    load("so", spatial_exit_hbm, so_ref)
+    parts = [pl.ds(i * width, width) for i in range(3)]
+    for i in range(3):
+        load(i, spatial_entry_hbm.at[:, parts[i]], se_ref.at[:, parts[i]])
 
     barrier = pltpu.get_barrier_semaphore()
     for k in range(1, frame_groups):
@@ -354,6 +360,26 @@
             {"frame": across(1 << step)},
         )
 
+    def send_owners(item):
+        first, count, index = item
+        step = bits - 1
+        slots = pl.ds(first, count)
+        for k in reversed(range(column_groups)):
+            owner = lax.rem(column_at + k, column_groups)
+            for far in (1, 0) if k else (1,):
+                frame_to = across(1 << step) if far else frame
+                choice = 1 - side[step] if far else side[step]
+                push(
+                    sums[step].at[slots, choice, owner],
+                    final.at[slots, far * column_groups + column_at],
+                    x_sem.at[0, index],
+                    x_sem.at[1, index],
+                    {"dp": clip(row_at, owner), "frame": frame_to},
+                )
+        for slot in range(first, first + count):
+            final[slot, column_at] = sums[step][slot, side[step], column_at]
+        sent.append((final.at[slots, pl.ds(0, 2 * column_groups - 1)], x_sem.at[0, index]))
+
     def halve(item, step):
         first, count, index = item
         half = frame_groups >> (step + 1)
@@ -361,40 +387,27 @@
         for slot in range(first, first + count):
             kept = sums[step][slot, pl.ds(side[step] * half, half)].astype(F32)
             total = kept + received[step][slot].astype(F32)
-            if step == bits - 1:
-                total = total * grad_factor
             sums[step + 1][slot] = total.astype(BF16)
-        if step < bits - 1:
+        if step < bits - 2:
             send_half(item, step + 1)
             return
-        sent.append((part.at[pl.ds(first, count), pl.ds(0, frame_groups - 1)], rs_sem.at[index]))
-        done = sums[bits]
+        sent.append((part.at[pl.ds(first, count), pl.ds(0, frame_groups - 2)], rs_sem.at[index]))
+        send_owners(item)
+
+    def settle(item):
+        first, count, index = item
+        drain(final.at[pl.ds(first, count), pl.ds(0, 2 * column_groups - 1)], x_sem.at[1, index])
         for slot in range(first, first + count):
-            for peer_column in column_peers():
-                push(
-                    done.at[slot, 0, peer_column],
-                    result(slot, column_at),
-                    x_sem.at[0, slot],
-                    x_sem.at[1, slot],
-                    {"dp": clip(row_at, peer_column)},
-                )
-            result(slot, column_at)[...] = done[slot, 0, column_at]
-            others = done.at[slot, 0, pl.ds(0, column_groups - 1)]
-            sent.append((others, x_sem.at[0, slot]))
-
-    def settle(item):
-        first, count, _ = item
-        for slot in range(first, first + count):
-            drain(sums[bits].at[slot, 0, pl.ds(0, column_groups - 1)], x_sem.at[1, slot])
+            out, start = outputs[slot]
+            for c in range(column_groups):
+                near, far = final[slot, c], final[slot, column_groups + c]
+                total = (near.astype(F32) + far.astype(F32)) * grad_factor
+                out[:, start + c * block : start + (c + 1) * block] = total.astype(BF16)
 
     outputs = [(temporalout_ref, 0)]
     outputs += [(temporalin_ref, i * width) for i in (2, 1, 0)]
     outputs += [(spatialout_ref, 0)]
     outputs += [(spatialin_ref, i * width) for i in (2, 1, 0)]
-
-    def result(slot, column):
-        out, start = outputs[slot]
-        return out.at[:, pl.ds(pl.multiple_of(start + column * block, block), block)]
 
     with jax.named_scope("a01_norm"):
         loads["frames"].wait()
@@ -405,19 +418,23 @@
         normed, s_inverse = normalize(tokens[...])
         s_normed[...] = normed
         s_low = normed.astype(BF16)
-        loads["se"].wait()
+        load("so", spatial_exit_hbm, so_ref)
         load("og", output_grad_hbm, og_send)
         load("te", temporal_entry_hbm, te_ref)
         load("to", temporal_exit_hbm, to_ref)
         load("joined", joined_hbm, joined_ref)
     columns = lax.broadcasted_iota(jnp.int32, (HEADS * rows, rows), 1)
-    attended, s_saved = attend(s_low, se_ref, columns < patches + bottles)
+    def enter(i):
+        loads[i].wait()
+
+
+    attended, s_saved = attend(s_low, se_ref, columns < patches + bottles, enter)
     with jax.named_scope("a02_states"):
         loads["so"].wait()
         states = (tokens[:patches] + dot(attended[:patches], so_ref[...], 1, 1)).astype(BF16)
         st_send[...] = states.astype(F32).reshape(frame_groups, group, model).astype(BF16)
+        pl.semaphore_wait(barrier, frame_groups + data_groups - 2)
     with jax.named_scope("a03_enter"):
-        pl.semaphore_wait(barrier, frame_groups + data_groups - 2)
         exchange_frames(st_send, st_recv, 0)
         loads["og"].wait()
         exchange_frames(og_send, og_recv, 1)
@@ -425,16 +442,20 @@
         s_att_shared = share(s_att_send, s_att, attended, False, 1)
 
     t_rows = frame_groups * group
+    with jax.named_scope("a04_turn"):
+        loads["te"].wait()
+        turned_te[...] = te_ref[...].T
+        turned_se[...] = se_ref[...].T
+    with jax.named_scope("a04_relays"):
+        relay(s_nl_shared)
+        relay(s_att_shared)
     with jax.named_scope("a05_waitst"):
         arrive_frames(st_recv, 0)
     with jax.named_scope("a06_tempfwd"):
         normed, t_inverse = normalize(st_recv[...].astype(F32).reshape(t_rows, model))
         t_normed[...] = normed
         t_low = normed.astype(BF16)
-        relay(s_nl_shared)
-        relay(s_att_shared)
         t_nl_shared = share(t_nl_send, t_nl, t_low, True, 2)
-        loads["te"].wait()
         shape = (HEADS * t_rows, t_rows)
         row_patch = lax.broadcasted_iota(jnp.int32, shape, 0) & (group - 1)
         column_patch = lax.broadcasted_iota(jnp.int32, shape, 1) & (group - 1)
@@ -453,7 +474,7 @@
     with jax.named_scope("a07_tempbwd"):
         loads["to"].wait()
         mixture_grad = backward_mixture(t_cot_low, to_ref, t_saved, keep_temporal)
-        state_grads = backward_inputs(mixture_grad, te_ref, t_cot, t_normed[...], t_inverse)
+        state_grads = backward_inputs(mixture_grad, turned_te, t_cot, t_normed[...], t_inverse)
         sg_send[...] = state_grads.reshape(frame_groups, group, model).astype(BF16)
         exchange_frames(sg_send, sg_recv, 2)
 
@@ -468,7 +489,8 @@
         )
         for i in (2, 1, 0):
             relay(t_shared[i])
-    temporal_exit_item, temporal_item = (0, 1, 0), (1, 3, 1)
+    temporal = [(slot, 1, slot) for slot in range(4)]
+    spatial = [(4 + slot, 1, 4 + slot) for slot in range(4)]
     with jax.named_scope("a09_waitsg"):
         arrive_frames(sg_recv, 2)
     cot_ref[:patches] = sg_recv[...].astype(F32).reshape(patches, model)
@@ -484,23 +506,22 @@
                 finish(t_c_shared)
             with jax.named_scope("b1_exit"):
                 gradient(0, t_c, t_att)
-                send_half(temporal_exit_item, 0)
-        if i == 1:
-            halve(temporal_exit_item, 0)
+                send_half(temporal[0], 0)
         if i == 0:
             with jax.named_scope("b2_w"):
                 finish(t_nl_shared)
-                for n in (2, 1, 0):
-                    finish(t_shared[n])
             with jax.named_scope("b2_entry"):
                 for slot in (1, 2, 3):
+                    finish(t_shared[3 - slot])
                     gradient(slot, t_nl, t_mg.at[3 - slot])
-                send_half(temporal_item, 0)
-
-    with jax.named_scope("b0_spatbwd"):
+                    send_half(temporal[slot], 0)
+                    if slot == 1:
+                        halve(temporal[0], 0)
+
+    with jax.named_scope("b3_spatbwd"):
         mixture_grad = backward_mixture(s_cot_low, so_ref, s_saved, keep_spatial)
-        halve(temporal_item, 0)
-        tokens_grad = backward_inputs(mixture_grad, se_ref, cot_ref[...], s_normed[...], s_inverse)
+    with jax.named_scope("b4_inputs"):
+        tokens_grad = backward_inputs(mixture_grad, turned_se, cot_ref[...], s_normed[...], s_inverse)
         frames_delta_ref[...] = tokens_grad[:patches].astype(BF16)
         bot_sum[0] = tokens_grad[patches : patches + bottles]
 
@@ -537,57 +558,47 @@
             store(bottle_delta_ref, bottle_delta_hbm)
 
     send_bottles(0)
-    spatial_a, spatial_b, spatial_c = (4, 2, 2), (6, 1, 3), (7, 1, 4)
+    with jax.named_scope("b5_halve"):
+        for slot in (1, 2, 3):
+            halve(temporal[slot], 0)
     finish(s_nl_shared)
     finish(s_att_shared)
-    with jax.named_scope("c1_w"):
+    with jax.named_scope("c0_w"):
         finish_direct(s_c_shared)
-        finish_direct(s_shared[2])
-    with jax.named_scope("c1_mm"):
+    with jax.named_scope("c0_mm"):
         gradient(4, s_c, s_att)
-        gradient(5, s_nl, s_mg.at[2])
-        send_half(spatial_a, 0)
-    with jax.named_scope("c3_w"):
-        finish_direct(s_shared[1])
-    with jax.named_scope("c3_mm"):
-        gradient(6, s_nl, s_mg.at[1])
-        send_half(spatial_b, 0)
-        halve(spatial_a, 0)
-    with jax.named_scope("c4_w"):
-        finish_direct(s_shared[0])
-    with jax.named_scope("c4_mm"):
-        gradient(7, s_nl, s_mg.at[0])
-        send_half(spatial_c, 0)
-        halve(spatial_b, 0)
-    with jax.named_scope("c5_halve"):
-        halve(temporal_exit_item, 1)
-        halve(spatial_c, 0)
-    for step in range(1, bits + 1):
+        send_half(spatial[0], 0)
+        add_bottles(0)
+    for n, i in enumerate((2, 1, 0)):
+        with jax.named_scope("c%d_w" % (n + 1)):
+            finish_direct(s_shared[i])
+        with jax.named_scope("c%d_mm" % (n + 1)):
+            gradient(5 + n, s_nl, s_mg.at[i])
+            send_half(spatial[n + 1], 0)
+        with jax.named_scope("c%d_halve" % (n + 1)):
+            halve(spatial[n], 0)
+    with jax.named_scope("c4_halve"):
+        halve(spatial[3], 0)
+    for step in range(1, bits - 1):
         with jax.named_scope("d%d_t" % step):
-            if step > 1 and step < bits:
-                halve(temporal_exit_item, step)
-            if step < bits:
-                halve(temporal_item, step)
-        if step < bits:
-            with jax.named_scope("d%d_a" % step):
-                add_bottles(step - 1)
-                halve(spatial_a, step)
-            with jax.named_scope("d%d_b" % step):
-                halve(spatial_b, step)
-            with jax.named_scope("d%d_c" % step):
-                halve(spatial_c, step)
-    add_bottles(bits - 1)
-    with jax.named_scope("e1_settle"):
-        settle(temporal_exit_item)
+            add_bottles(step)
+            for it in temporal:
+                halve(it, step)
+        for n, it in enumerate(spatial):
+            with jax.named_scope("d%d_s%d" % (step, n)):
+                halve(it, step)
+    with jax.named_scope("e1_t"):
+        add_bottles(bits - 1)
+        for it in temporal:
+            settle(it)
         store(temporalout_ref, temporalout_hbm)
-        settle(temporal_item)
         store(temporalin_ref, temporalin_hbm)
-        settle(spatial_a)
-        store(spatialout_ref, spatialout_hbm)
-        settle(spatial_b)
-        settle(spatial_c)
-        store(spatialin_ref, spatialin_hbm)
-    with jax.named_scope("e2_drain"):
+    for n, it in enumerate(spatial):
+        with jax.named_scope("e2_s%d" % n):
+            settle(it)
+    store(spatialout_ref, spatialout_hbm)
+    store(spatialin_ref, spatialin_hbm)
+    with jax.named_scope("e3_drain"):
         for view, sem in sent:
             drain(view, sem)
         for copy in bottle_copies:
@@ -622,7 +633,7 @@
     group = patches // frame_groups
     assert group & (group - 1) == 0
     assert frame_groups & (frame_groups - 1) == 0 and data_groups & (data_groups - 1) == 0
-    assert entry_width == 3 * exit_width
+    assert entry_width == 3 * exit_width and frame_groups >= 4
     bits = frame_groups.bit_length() - 1
     row_groups = 1 << ((data_groups.bit_length() - 1) // 2)
     column_groups = data_groups // row_groups
@@ -671,6 +682,8 @@
             pltpu.VMEM(spatial_exit.shape, BF16),
             pltpu.VMEM(temporal_entry.shape, BF16),
             pltpu.VMEM(temporal_exit.shape, BF16),
+            pltpu.VMEM(spatial_entry.shape[::-1], BF16),
+            pltpu.VMEM(temporal_entry.shape[::-1], BF16),
             *[pltpu.VMEM(out.shape, BF16) for out in out_shape],
             pltpu.VMEM((rows, model), F32),
             pltpu.VMEM((rows, model), F32),
@@ -686,17 +699,18 @@
             *gather_set(sent_rows),
             *gather_set(t_rows),
             pltpu.VMEM((8, frame_groups, column_groups, owned, block), BF16),
+            pltpu.VMEM((8, 2 * column_groups, owned, block), BF16),
             *[
                 pltpu.VMEM((8, frame_groups >> s, column_groups, owned, block), BF16)
-                for s in range(1, bits + 1)
+                for s in range(1, bits)
             ]
             * 2,
-            pltpu.SemaphoreType.DMA((8,)),
+            pltpu.SemaphoreType.DMA((10,)),
             pltpu.SemaphoreType.DMA((6,)),
             pltpu.SemaphoreType.DMA((2, 3)),
             pltpu.SemaphoreType.DMA((3, 12)),
-            pltpu.SemaphoreType.DMA((5, bits)),
-            pltpu.SemaphoreType.DMA((5,)),
+            pltpu.SemaphoreType.DMA((8, bits - 1)),
+            pltpu.SemaphoreType.DMA((8,)),
             pltpu.SemaphoreType.DMA((2, 8)),
             pltpu.SemaphoreType.DMA((2, bits)),
         ],

time: 56.7 us -> 51.8 us (0.914)
  Pallas kernels: 55.9 us -> 51 us
    pallas_call x1, Pallas kernels: 54.1 us -> 49.2 us  [per_device(): pl.pallas_call(functools.partial(kernel, frame_groups, row_groups, column...]
where the time goes in v3:
time: 51.8 us; the launch traced here: 51.7 us
  Pallas kernels  51 us (98%)
  between operations  0.64 us (1%)
    pallas_call x1, Pallas kernels, per_device(): pl.pallas_call(functools.partial(kernel, frame_groups, row_groups, column...  49.2 us
    pallas_call x1, Pallas kernels, per_device(): pl.pallas_call(hand_over, out_shape=[jax.ShapeDtypeStruct(out.shape, out....  1.79 us

profile of v3, /device:TPU:0, one launch (start us, length us, event | category | flops | bytes accessed | tf_op | source)
XLA Modules:
  0.0 51.7 jit_solution(8560518212592313128)
XLA Ops:
  0.6 49.2 %shard_map.127 = (bf16[64,1024]{1,0:T(8,128)(2,1)}, bf16[4,1024]{1,0:T(4,128)(2,1)}, bf16[32,1536]{1,0:T(8,128)(2,1)}, bf16[32,512]{1,0:T(8,128)(2,1)}, bf16[32,...) custom-call(bf16[64,1024]{1,0:T(8,128)(2,1)} %bitcast.6, bf16[4,1024]{1,0:T(4,128)(2,1)} %bitcast.8, ...), custom_call_target="tpu_custom_call" | custom-call | tf_op jit(solution)/shard_map/pallas_call | solution.py:671
  49.9 1.8 %shard_map.128 = (bf16[64,1024]{1,0:T(8,128)(2,1)}, bf16[4,1024]{1,0:T(4,128)(2,1)}, bf16[32,1536]{1,0:T(8,128)(2,1)}, bf16[32,512]{1,0:T(8,128)(2,1)}, bf16[32,...) custom-call(bf16[64,1024]{1,0:T(8,128)(2,1)} %get-tuple-element.18.refs_0_, bf16[4,1024]{1,0:T(4,128)(2,1)} %get-tuple-element.19.refs_1_, ...), custom_call_target="tpu_custom_call" | custom-call | tf_op jit(solution)/shard_map/pallas_call | solution.py:730

commit v4 on v3

--- a/solution.py
+++ b/solution.py
@@ -9,6 +9,7 @@
 from jax.sharding import PartitionSpec as P
 
 HEADS = 8
+LANES = 128
 EPSILON = 1e-05
 MESH = pl.DeviceIdType.MESH
 F32 = jnp.float32
@@ -27,24 +28,30 @@
     return centred * inverse, inverse
 
 
-def head_masks(width, dtype):
+def head_masks(heads, width, dtype):
     lanes = lax.broadcasted_iota(jnp.int32, (1, width), 1)
-    size = width // HEADS
+    size = width // heads
     return [
         jnp.where((lanes >= h * size) & (lanes < (h + 1) * size), 1.0, 0.0).astype(dtype)
-        for h in range(HEADS)
+        for h in range(heads)
     ]
 
 
-def stack_heads(rows):
-    return jnp.concatenate([rows * m for m in head_masks(rows.shape[1], rows.dtype)], axis=0)
-
-
-def merge_heads(stacked):
-    count = stacked.shape[0] // HEADS
-    masks = head_masks(stacked.shape[1], stacked.dtype)
+def split(rows):
+    width = rows.shape[1]
+    lanes = max(LANES, width // HEADS)
+    return [rows[:, i : i + lanes] for i in range(0, width, lanes)]
+
+
+def stack_heads(rows, heads):
+    return jnp.concatenate([rows * m for m in head_masks(heads, rows.shape[1], rows.dtype)], axis=0)
+
+
+def merge_heads(stacked, heads):
+    count = stacked.shape[0] // heads
+    masks = head_masks(heads, stacked.shape[1], stacked.dtype)
     total = stacked[:count] * masks[0]
-    for h in range(1, HEADS):
+    for h in range(1, heads):
         total = total + stacked[h * count : (h + 1) * count] * masks[h]
     return total
 
@@ -55,32 +62,45 @@
     for i in range(3):
         ready(i)
         parts.append(dot(normed_low, entry_ref[:, i * width : (i + 1) * width]).astype(BF16))
-    queries, key_rows, values = parts
     factor = 1.0 / math.sqrt(width // HEADS)
-    query_stack = stack_heads(queries)
-    scores = dot(query_stack, key_rows, 1, 1) * factor
-    scores = jnp.where(mask, scores, -1e30)
-    scores = scores - jnp.max(scores, axis=-1, keepdims=True)
-    expon = jnp.where(mask, jnp.exp(scores), 0.0)
-    weights = expon / jnp.sum(expon, axis=-1, keepdims=True)
-    weights_low = weights.astype(BF16)
-    attended = merge_heads(dot(weights_low, values)).astype(BF16)
-    return attended, (query_stack, key_rows, values, weights, weights_low)
+    saved, attended = [], []
+    for queries, key_rows, values in zip(*map(split, parts)):
+        heads = HEADS * queries.shape[1] // width
+        query_stack = stack_heads(queries, heads)
+        scores = dot(query_stack, key_rows, 1, 1) * factor
+        here = mask(scores.shape)
+        scores = jnp.where(here, scores, -1e30)
+        scores = scores - jnp.max(scores, axis=-1, keepdims=True)
+        expon = jnp.where(here, jnp.exp(scores), 0.0)
+        weights = expon / jnp.sum(expon, axis=-1, keepdims=True)
+        weights_low = weights.astype(BF16)
+        attended.append(merge_heads(dot(weights_low, values), heads).astype(BF16))
+        saved.append((query_stack, key_rows, values, weights, weights_low))
+    return jnp.concatenate(attended, axis=1), saved
 
 
 def backward_mixture(cotangent, exit_ref, saved, emit):
-    query_stack, key_rows, values, weights, weights_low = saved
-    factor = 1.0 / math.sqrt(values.shape[1] // HEADS)
-    attended_grad = dot(cotangent, exit_ref[...]).astype(BF16)
-    grad_stack = stack_heads(attended_grad)
-    values_grad = dot(weights_low, grad_stack, 0, 0).astype(BF16)
+    width = exit_ref.shape[1]
+    factor = 1.0 / math.sqrt(width // HEADS)
+    attended_grad = split(dot(cotangent, exit_ref[...]).astype(BF16))
+    heads = HEADS * attended_grad[0].shape[1] // width
+    grad_stacks = [stack_heads(g, heads) for g in attended_grad]
+    values_grad = jnp.concatenate(
+        [dot(s[4], g, 0, 0).astype(BF16) for s, g in zip(saved, grad_stacks)], axis=1
+    )
     emit(2, values_grad)
-    softmax_grad = dot(grad_stack, values, 1, 1)
-    centre = jnp.sum(weights * softmax_grad, axis=-1, keepdims=True)
-    scores_grad = (weights * (softmax_grad - centre) * factor).astype(BF16)
-    keys_grad = dot(scores_grad, query_stack, 0, 0).astype(BF16)
+    scores_grads = []
+    for (_, _, values, weights, _), grad_stack in zip(saved, grad_stacks):
+        softmax_grad = dot(grad_stack, values, 1, 1)
+        centre = jnp.sum(weights * softmax_grad, axis=-1, keepdims=True)
+        scores_grads.append((weights * (softmax_grad - centre) * factor).astype(BF16))
+    keys_grad = jnp.concatenate(
+        [dot(g, s[0], 0, 0).astype(BF16) for s, g in zip(saved, scores_grads)], axis=1
+    )
     emit(1, keys_grad)
-    queries_grad = merge_heads(dot(scores_grad, key_rows)).astype(BF16)
+    queries_grad = jnp.concatenate(
+        [merge_heads(dot(g, s[1]), heads).astype(BF16) for s, g in zip(saved, scores_grads)], axis=1
+    )
     emit(0, queries_grad)
     return jnp.concatenate([queries_grad, keys_grad, values_grad], axis=1)
 
@@ -108,12 +128,12 @@
     spatial_exit_hbm,
     temporal_entry_hbm,
     temporal_exit_hbm,
-    frames_delta_hbm,
-    bottle_delta_hbm,
-    spatialin_hbm,
-    spatialout_hbm,
-    temporalin_hbm,
-    temporalout_hbm,
+    frames_delta_ref,
+    bottle_delta_ref,
+    spatialin_ref,
+    spatialout_ref,
+    temporalin_ref,
+    temporalout_ref,
     frames_ref,
     bottle_ref,
     og_send,
@@ -124,12 +144,6 @@
     to_ref,
     turned_se,
     turned_te,
-    frames_delta_ref,
-    bottle_delta_ref,
-    spatialin_ref,
-    spatialout_ref,
-    temporalin_ref,
-    temporalout_ref,
     tokens,
     cot_ref,
     s_normed,
@@ -139,6 +153,8 @@
     st_recv,
     sg_send,
     sg_recv,
+    at_send,
+    at_recv,
     bot_sum,
     bot_recv,
     s_nl_send,
@@ -165,7 +181,6 @@
     sums = (part,) + tuple(tail[1 + bits : 2 * bits])
     (
         load_sem,
-        out_sem,
         f_sem,
         d_sem,
         r_sem,
@@ -404,6 +419,9 @@
                 total = (near.astype(F32) + far.astype(F32)) * grad_factor
                 out[:, start + c * block : start + (c + 1) * block] = total.astype(BF16)
 
+    def flat(ref, count):
+        return ref[...].astype(F32).reshape(count, ref.shape[2]).astype(BF16)
+
     outputs = [(temporalout_ref, 0)]
     outputs += [(temporalin_ref, i * width) for i in (2, 1, 0)]
     outputs += [(spatialout_ref, 0)]
@@ -423,12 +441,14 @@
         load("te", temporal_entry_hbm, te_ref)
         load("to", temporal_exit_hbm, to_ref)
         load("joined", joined_hbm, joined_ref)
-    columns = lax.broadcasted_iota(jnp.int32, (HEADS * rows, rows), 1)
+    def real_rows(shape):
+        return lax.broadcasted_iota(jnp.int32, shape, 1) < patches + bottles
+
     def enter(i):
         loads[i].wait()
 
 
-    attended, s_saved = attend(s_low, se_ref, columns < patches + bottles, enter)
+    attended, s_saved = attend(s_low, se_ref, real_rows, enter)
     with jax.named_scope("a02_states"):
         loads["so"].wait()
         states = (tokens[:patches] + dot(attended[:patches], so_ref[...], 1, 1)).astype(BF16)
@@ -438,6 +458,7 @@
         exchange_frames(st_send, st_recv, 0)
         loads["og"].wait()
         exchange_frames(og_send, og_recv, 1)
+        t_c_shared = share(t_c_send, t_c, flat(og_send, patches), True, 4)
         s_nl_shared = share(s_nl_send, s_nl, s_low, True, 0)
         s_att_shared = share(s_att_send, s_att, attended, False, 1)
 
@@ -447,29 +468,30 @@
         turned_te[...] = te_ref[...].T
         turned_se[...] = se_ref[...].T
     with jax.named_scope("a04_relays"):
-        relay(s_nl_shared)
-        relay(s_att_shared)
+        relay(t_c_shared)
+    def same_patch(shape):
+        row_patch = lax.broadcasted_iota(jnp.int32, shape, 0) & (group - 1)
+        column_patch = lax.broadcasted_iota(jnp.int32, shape, 1) & (group - 1)
+        return row_patch == column_patch
+
     with jax.named_scope("a05_waitst"):
         arrive_frames(st_recv, 0)
     with jax.named_scope("a06_tempfwd"):
         normed, t_inverse = normalize(st_recv[...].astype(F32).reshape(t_rows, model))
         t_normed[...] = normed
         t_low = normed.astype(BF16)
-        t_nl_shared = share(t_nl_send, t_nl, t_low, True, 2)
-        shape = (HEADS * t_rows, t_rows)
-        row_patch = lax.broadcasted_iota(jnp.int32, shape, 0) & (group - 1)
-        column_patch = lax.broadcasted_iota(jnp.int32, shape, 1) & (group - 1)
-        attended, t_saved = attend(t_low, te_ref, row_patch == column_patch)
-        t_att_shared = share(t_att_send, t_att, attended, False, 3)
+        t_nl_shared = share_direct(t_nl_send, t_nl, t_low, True, 2)
+        attended, t_saved = attend(t_low, te_ref, same_patch)
+        at_send[...] = attended.astype(F32).reshape(at_send.shape).astype(BF16)
+        exchange_frames(at_send, at_recv, 3)
     with jax.named_scope("a06_waitog"):
         arrive_frames(og_recv, 1)
     t_cot = og_recv[...].astype(F32).reshape(t_rows, model)
     t_cot_low = t_cot.astype(BF16)
-    t_c_shared = share(t_c_send, t_c, t_cot_low, True, 4)
     t_shared = {}
 
     def keep_temporal(i, value):
-        t_shared[i] = share(t_mg_send.at[i], t_mg.at[i], value, False, 5 + i)
+        t_shared[i] = share_direct(t_mg_send.at[i], t_mg.at[i], value, False, 5 + i)
 
     with jax.named_scope("a07_tempbwd"):
         loads["to"].wait()
@@ -479,16 +501,15 @@
         exchange_frames(sg_send, sg_recv, 2)
 
     with jax.named_scope("a08_relays"):
-        relay(t_nl_shared)
-        relay(t_att_shared)
-        relay(t_c_shared)
+        relay(s_nl_shared)
+        relay(s_att_shared)
+        arrive_frames(at_recv, 3)
+        t_att_shared = share_direct(t_att_send, t_att, flat(at_recv, patches), False, 3)
         cot_ref[patches:] = jnp.zeros((rows - patches, model), F32)
         loads["joined"].wait()
         cot_ref[patches : patches + bottles] = (
             (joined_ref[...].astype(F32) / frame_groups).astype(BF16).astype(F32)
         )
-        for i in (2, 1, 0):
-            relay(t_shared[i])
     temporal = [(slot, 1, slot) for slot in range(4)]
     spatial = [(4 + slot, 1, 4 + slot) for slot in range(4)]
     with jax.named_scope("a09_waitsg"):
@@ -500,23 +521,16 @@
 
     def keep_spatial(i, value):
         s_shared[i] = share_direct(s_mg_send.at[i], s_mg.at[i], value, False, 9 + i)
-        if i == 2:
+        if i == 0:
             with jax.named_scope("b1_w"):
-                finish(t_att_shared)
-                finish(t_c_shared)
-            with jax.named_scope("b1_exit"):
-                gradient(0, t_c, t_att)
-                send_half(temporal[0], 0)
-        if i == 0:
-            with jax.named_scope("b2_w"):
-                finish(t_nl_shared)
-            with jax.named_scope("b2_entry"):
+                finish_direct(t_nl_shared)
+                finish_direct(t_shared[2])
+            with jax.named_scope("b1_entry"):
                 for slot in (1, 2, 3):
-                    finish(t_shared[3 - slot])
+                    if slot > 1:
+                        finish_direct(t_shared[3 - slot])
                     gradient(slot, t_nl, t_mg.at[3 - slot])
                     send_half(temporal[slot], 0)
-                    if slot == 1:
-                        halve(temporal[0], 0)
 
     with jax.named_scope("b3_spatbwd"):
         mixture_grad = backward_mixture(s_cot_low, so_ref, s_saved, keep_spatial)
@@ -524,15 +538,6 @@
         tokens_grad = backward_inputs(mixture_grad, turned_se, cot_ref[...], s_normed[...], s_inverse)
         frames_delta_ref[...] = tokens_grad[:patches].astype(BF16)
         bot_sum[0] = tokens_grad[patches : patches + bottles]
-
-    stores = []
-
-    def store(src, dst):
-        copy = pltpu.make_async_copy(src, dst, out_sem.at[len(stores)])
-        copy.start()
-        stores.append(copy)
-
-    store(frames_delta_ref, frames_delta_hbm)
 
     bottle_copies = []
 
@@ -555,12 +560,22 @@
             send_bottles(step + 1)
         else:
             bottle_delta_ref[...] = total.astype(BF16)
-            store(bottle_delta_ref, bottle_delta_hbm)
 
     send_bottles(0)
     with jax.named_scope("b5_halve"):
         for slot in (1, 2, 3):
             halve(temporal[slot], 0)
+    with jax.named_scope("b6_w"):
+        finish(t_c_shared)
+        finish_direct(t_att_shared)
+    with jax.named_scope("b6_exit"):
+        gradient(0, t_c, t_att)
+        send_half(temporal[0], 0)
+    with jax.named_scope("b7_halve"):
+        add_bottles(0)
+        halve(temporal[1], 1)
+        halve(temporal[0], 0)
+        halve(temporal[2], 1)
     finish(s_nl_shared)
     finish(s_att_shared)
     with jax.named_scope("c0_w"):
@@ -568,7 +583,6 @@
     with jax.named_scope("c0_mm"):
         gradient(4, s_c, s_att)
         send_half(spatial[0], 0)
-        add_bottles(0)
     for n, i in enumerate((2, 1, 0)):
         with jax.named_scope("c%d_w" % (n + 1)):
             finish_direct(s_shared[i])
@@ -577,34 +591,32 @@
             send_half(spatial[n + 1], 0)
         with jax.named_scope("c%d_halve" % (n + 1)):
             halve(spatial[n], 0)
+            if n == 1:
+                halve(temporal[3], 1)
     with jax.named_scope("c4_halve"):
         halve(spatial[3], 0)
+        halve(temporal[0], 1)
     for step in range(1, bits - 1):
         with jax.named_scope("d%d_t" % step):
             add_bottles(step)
-            for it in temporal:
-                halve(it, step)
+            if step > 1:
+                for it in temporal:
+                    halve(it, step)
         for n, it in enumerate(spatial):
             with jax.named_scope("d%d_s%d" % (step, n)):
                 halve(it, step)
     with jax.named_scope("e1_t"):
         add_bottles(bits - 1)
-        for it in temporal:
+        for it in temporal[1:] + temporal[:1]:
             settle(it)
-        store(temporalout_ref, temporalout_hbm)
-        store(temporalin_ref, temporalin_hbm)
     for n, it in enumerate(spatial):
         with jax.named_scope("e2_s%d" % n):
             settle(it)
-    store(spatialout_ref, spatialout_hbm)
-    store(spatialin_ref, spatialin_hbm)
     with jax.named_scope("e3_drain"):
         for view, sem in sent:
             drain(view, sem)
         for copy in bottle_copies:
             copy.wait_send()
-        for copy in stores:
-            copy.wait()
 
 
 def hand_over(*refs):
@@ -658,7 +670,7 @@
         ]
 
     moved = pltpu.VMEM((frame_groups, group, model), BF16)
-    hbm = pl.BlockSpec(memory_space=pl.ANY)
+    hbm = pl.BlockSpec(memory_space=pltpu.HBM)
     vmem = pl.BlockSpec(memory_space=pltpu.VMEM)
     out_shape = (
         jax.ShapeDtypeStruct((patches, model), BF16),
@@ -672,7 +684,7 @@
         functools.partial(kernel, frame_groups, row_groups, column_groups, grad_factor),
         out_shape=out_shape,
         in_specs=[hbm] * 8,
-        out_specs=[hbm] * 6,
+        out_specs=[vmem] * 6,
         scratch_shapes=[
             pltpu.VMEM((patches, model), BF16),
             pltpu.VMEM((bottles, model), BF16),
@@ -684,7 +696,6 @@
             pltpu.VMEM(temporal_exit.shape, BF16),
             pltpu.VMEM(spatial_entry.shape[::-1], BF16),
             pltpu.VMEM(temporal_entry.shape[::-1], BF16),
-            *[pltpu.VMEM(out.shape, BF16) for out in out_shape],
             pltpu.VMEM((rows, model), F32),
             pltpu.VMEM((rows, model), F32),
             pltpu.VMEM((rows, model), F32),
@@ -694,6 +705,7 @@
             moved,
             moved,
             moved,
+            *[pltpu.VMEM((frame_groups, group, exit_width), BF16)] * 2,
             pltpu.VMEM((bits, bottles, model), F32),
             pltpu.VMEM((bits, bottles, model), F32),
             *gather_set(sent_rows),
@@ -706,8 +718,7 @@
             ]
             * 2,
             pltpu.SemaphoreType.DMA((10,)),
-            pltpu.SemaphoreType.DMA((6,)),
-            pltpu.SemaphoreType.DMA((2, 3)),
+            pltpu.SemaphoreType.DMA((2, 4)),
             pltpu.SemaphoreType.DMA((3, 12)),
             pltpu.SemaphoreType.DMA((8, bits - 1)),
             pltpu.SemaphoreType.DMA((8,)),
@@ -715,24 +726,29 @@
             pltpu.SemaphoreType.DMA((2, bits)),
         ],
         compiler_params=pltpu.CompilerParams(
-            collective_id=0, has_side_effects=True, vmem_limit_bytes=61 * 1024 * 1024
+            collective_id=0, has_side_effects=True, vmem_limit_bytes=40 * 1024 * 1024
         ),
     )(
-        frames_in.reshape(patches, model),
-        bottleneck.reshape(bottles, model),
-        output_grad.reshape(frame_groups, group, model),
-        joined_grad.reshape(bottles, model),
-        spatial_entry,
-        spatial_exit,
-        temporal_entry,
-        temporal_exit,
+        *[
+            pltpu.with_memory_space_constraint(x, pltpu.HBM)
+            for x in (
+                frames_in.reshape(patches, model),
+                bottleneck.reshape(bottles, model),
+                output_grad.reshape(frame_groups, group, model),
+                joined_grad.reshape(bottles, model),
+                spatial_entry,
+                spatial_exit,
+                temporal_entry,
+                temporal_exit,
+            )
+        ]
     )
     outs = pl.pallas_call(
         hand_over,
         out_shape=[jax.ShapeDtypeStruct(out.shape, out.dtype) for out in outs],
         in_specs=[vmem] * len(outs),
         out_specs=[vmem] * len(outs),
-        compiler_params=pltpu.CompilerParams(vmem_limit_bytes=61 * 1024 * 1024),
+        compiler_params=pltpu.CompilerParams(vmem_limit_bytes=40 * 1024 * 1024),
     )(*outs)
     return (outs[0].reshape(frames_in.shape), outs[1].reshape(bottleneck.shape), *outs[2:])
 

time: 51.8 us -> 47.3 us (0.913)
  Pallas kernels: 51 us -> 46.5 us
    pallas_call x1, Pallas kernels: 49.2 us -> 45.8 us  [per_device(): pl.pallas_call(functools.partial(kernel, frame_groups, row_groups, column...]
    pallas_call x1, Pallas kernels: 1.79 us -> 0.76 us  [per_device(): pl.pallas_call(hand_over, out_shape=[jax.ShapeDtypeStruct(out.shape, out....]
where the time goes in v4:
time: 47.3 us; the launch traced here: 47.2 us
  Pallas kernels  46.5 us (98%)
  between operations  0.64 us (1%)
    pallas_call x1, Pallas kernels, per_device(): pl.pallas_call(functools.partial(kernel, frame_groups, row_groups, column...  45.8 us

profile of v4, /device:TPU:0, one launch (start us, length us, event | category | flops | bytes accessed | tf_op | source)
XLA Modules:
  0.0 47.2 jit_solution(2605600617554128006)
XLA Ops:
  0.6 45.8 %shard_map.127 = (bf16[64,1024]{1,0:T(8,128)(2,1)S(1)}, bf16[4,1024]{1,0:T(4,128)(2,1)S(1)}, bf16[32,1536]{1,0:T(8,128)(2,1)S(1)}, bf16[32,512]{1,0:T(8,128)(2,1...) custom-call(bf16[64,1024]{1,0:T(8,128)(2,1)} %bitcast.6, bf16[4,1024]{1,0:T(4,128)(2,1)} %bitcast.8, ...), custom_call_target="tpu_custom_call" | custom-call | tf_op jit(solution)/shard_map/pallas_call | solution.py:683
  46.4 0.8 %shard_map.128 = (bf16[64,1024]{1,0:T(8,128)(2,1)}, bf16[4,1024]{1,0:T(4,128)(2,1)}, bf16[32,1536]{1,0:T(8,128)(2,1)}, bf16[32,512]{1,0:T(8,128)(2,1)}, bf16[32,...) custom-call(bf16[64,1024]{1,0:T(8,128)(2,1)S(1)} %get-tuple-element.18.refs_0_, bf16[4,1024]{1,0:T(4,128)(2,1)S(1)} %get-tuple-element.19.refs_1_, ...), custom_call_target="tpu_custom_call" | custom-call | tf_op jit(solution)/shard_map/pallas_call | solution.py:746

commit v5 on v4

--- a/solution.py
+++ b/solution.py
@@ -183,9 +183,11 @@
         load_sem,
         f_sem,
         d_sem,
+        dr_sem,
         r_sem,
         rs_sem,
         x_sem,
+        xs_sem,
         b_sem,
     ) = tail[2 * bits :]
     frame = lax.axis_index("frame")
@@ -251,8 +253,9 @@
                 peer = peer + (1 << s) * (1 - 2 * side[s])
         return peer
 
-    def exchange_frames(send, dst, phase):
-        for k in reversed(range(1, frame_groups)):
+    def exchange_frames(send, dst, phase, far_first=True):
+        order = range(1, frame_groups)
+        for k in reversed(order) if far_first else order:
             peer = across(k)
             push(
                 send.at[peer],
@@ -281,6 +284,9 @@
         for i in range(count):
             dst[i] = value[:kept, i * size : (i + 1) * size]
 
+    def send_slot(phase):
+        return phase if phase < 5 else 5 if phase < 8 else 6 if phase == 8 else 7
+
     def share(send, dst, value, by_row, phase):
         put_blocks(send, value)
         mine = row_at if by_row else column_at
@@ -288,26 +294,26 @@
             push(
                 send.at[peer_row if by_row else column_at],
                 dst.at[data],
-                d_sem.at[0, phase],
-                d_sem.at[1 if by_row else 2, phase],
+                d_sem.at[send_slot(phase)],
+                dr_sem.at[phase if by_row else 12 + min(phase, 2)],
                 {"dp": clip(peer_row, column_at)},
             )
         for peer_column in column_peers():
             push(
                 send.at[row_at if by_row else peer_column],
                 dst.at[data],
-                d_sem.at[0, phase],
-                d_sem.at[2 if by_row else 1, phase],
+                d_sem.at[send_slot(phase)],
+                dr_sem.at[12 + min(phase, 2) if by_row else phase],
                 {"dp": clip(row_at, peer_column)},
             )
         dst[data] = send[mine]
-        sent.append((dst.at[pl.ds(0, data_groups - 1)], d_sem.at[0, phase]))
+        sent.append((dst.at[pl.ds(0, data_groups - 1)], d_sem.at[send_slot(phase)]))
         return dst, by_row, phase
 
     def relay(shared):
         dst, by_row, phase = shared
         first = (row_groups if by_row else column_groups) - 1
-        drain(dst.at[pl.ds(0, first)], d_sem.at[1, phase])
+        drain(dst.at[pl.ds(0, first)], dr_sem.at[phase])
         for peer_row in row_peers():
             for peer_column in column_peers():
                 source = clip(peer_row, column_at) if by_row else clip(row_at, peer_column)
@@ -315,15 +321,15 @@
                 push(
                     dst.at[source],
                     dst.at[source],
-                    d_sem.at[0, phase],
-                    d_sem.at[2, phase],
+                    d_sem.at[send_slot(phase)],
+                    dr_sem.at[12 + min(phase, 2)],
                     {"dp": target},
                 )
 
     def finish(shared):
         dst, by_row, phase = shared
         first = (row_groups if by_row else column_groups) - 1
-        drain(dst.at[pl.ds(0, data_groups - 1 - first)], d_sem.at[2, phase])
+        drain(dst.at[pl.ds(0, data_groups - 1 - first)], dr_sem.at[12 + min(phase, 2)])
 
     def share_direct(send, dst, value, by_row, phase):
         put_blocks(send, value)
@@ -333,17 +339,18 @@
             push(
                 send.at[peer_row if by_row else peer_column],
                 dst.at[data],
-                d_sem.at[0, phase],
-                d_sem.at[1, phase],
+                d_sem.at[send_slot(phase)],
+                dr_sem.at[phase],
                 {"dp": clip(peer_row, peer_column)},
             )
         dst[data] = send[row_at if by_row else column_at]
-        sent.append((dst.at[pl.ds(0, data_groups - 1)], d_sem.at[0, phase]))
+        if send_slot(phase) not in (5, 7):
+            sent.append((dst.at[pl.ds(0, data_groups - 1)], d_sem.at[send_slot(phase)]))
         return dst, by_row, phase
 
     def finish_direct(shared):
         dst, _, phase = shared
-        drain(dst.at[pl.ds(0, data_groups - 1)], d_sem.at[1, phase])
+        drain(dst.at[pl.ds(0, data_groups - 1)], dr_sem.at[phase])
 
     def gradient(slot, left, right):
         def product_of(low, high):
@@ -370,7 +377,7 @@
         push(
             sums[step].at[slots, pl.ds((1 - side[step]) * half, half)],
             received[step].at[slots],
-            rs_sem.at[index],
+            rs_sem,
             r_sem.at[index, step],
             {"frame": across(1 << step)},
         )
@@ -387,13 +394,12 @@
                 push(
                     sums[step].at[slots, choice, owner],
                     final.at[slots, far * column_groups + column_at],
-                    x_sem.at[0, index],
-                    x_sem.at[1, index],
+                    xs_sem,
+                    x_sem.at[index],
                     {"dp": clip(row_at, owner), "frame": frame_to},
                 )
         for slot in range(first, first + count):
             final[slot, column_at] = sums[step][slot, side[step], column_at]
-        sent.append((final.at[slots, pl.ds(0, 2 * column_groups - 1)], x_sem.at[0, index]))
 
     def halve(item, step):
         first, count, index = item
@@ -406,12 +412,11 @@
         if step < bits - 2:
             send_half(item, step + 1)
             return
-        sent.append((part.at[pl.ds(first, count), pl.ds(0, frame_groups - 2)], rs_sem.at[index]))
         send_owners(item)
 
     def settle(item):
         first, count, index = item
-        drain(final.at[pl.ds(first, count), pl.ds(0, 2 * column_groups - 1)], x_sem.at[1, index])
+        drain(final.at[pl.ds(first, count), pl.ds(0, 2 * column_groups - 1)], x_sem.at[index])
         for slot in range(first, first + count):
             out, start = outputs[slot]
             for c in range(column_groups):
@@ -457,7 +462,7 @@
     with jax.named_scope("a03_enter"):
         exchange_frames(st_send, st_recv, 0)
         loads["og"].wait()
-        exchange_frames(og_send, og_recv, 1)
+        exchange_frames(og_send, og_recv, 1, far_first=False)
         t_c_shared = share(t_c_send, t_c, flat(og_send, patches), True, 4)
         s_nl_shared = share(s_nl_send, s_nl, s_low, True, 0)
         s_att_shared = share(s_att_send, s_att, attended, False, 1)
@@ -512,6 +517,14 @@
         )
     temporal = [(slot, 1, slot) for slot in range(4)]
     spatial = [(4 + slot, 1, 4 + slot) for slot in range(4)]
+    def reduce_entry(slot):
+        finish_direct(t_shared[3 - slot])
+        gradient(slot, t_nl, t_mg.at[3 - slot])
+        send_half(temporal[slot], 0)
+
+    with jax.named_scope("b1_first"):
+        finish_direct(t_nl_shared)
+        reduce_entry(1)
     with jax.named_scope("a09_waitsg"):
         arrive_frames(sg_recv, 2)
     cot_ref[:patches] = sg_recv[...].astype(F32).reshape(patches, model)
@@ -521,17 +534,16 @@
 
     def keep_spatial(i, value):
         s_shared[i] = share_direct(s_mg_send.at[i], s_mg.at[i], value, False, 9 + i)
+        if i == 2:
+            with jax.named_scope("b3_third"):
+                halve(temporal[2], 0)
+                reduce_entry(3)
         if i == 0:
-            with jax.named_scope("b1_w"):
-                finish_direct(t_nl_shared)
-                finish_direct(t_shared[2])
-            with jax.named_scope("b1_entry"):
-                for slot in (1, 2, 3):
-                    if slot > 1:
-                        finish_direct(t_shared[3 - slot])
-                    gradient(slot, t_nl, t_mg.at[3 - slot])
-                    send_half(temporal[slot], 0)
-
+            halve(temporal[3], 0)
+
+    with jax.named_scope("b2_second"):
+        halve(temporal[1], 0)
+        reduce_entry(2)
     with jax.named_scope("b3_spatbwd"):
         mixture_grad = backward_mixture(s_cot_low, so_ref, s_saved, keep_spatial)
     with jax.named_scope("b4_inputs"):
@@ -562,9 +574,6 @@
             bottle_delta_ref[...] = total.astype(BF16)
 
     send_bottles(0)
-    with jax.named_scope("b5_halve"):
-        for slot in (1, 2, 3):
-            halve(temporal[slot], 0)
     with jax.named_scope("b6_w"):
         finish(t_c_shared)
         finish_direct(t_att_shared)
@@ -575,7 +584,6 @@
         add_bottles(0)
         halve(temporal[1], 1)
         halve(temporal[0], 0)
-        halve(temporal[2], 1)
     finish(s_nl_shared)
     finish(s_att_shared)
     with jax.named_scope("c0_w"):
@@ -583,6 +591,7 @@
     with jax.named_scope("c0_mm"):
         gradient(4, s_c, s_att)
         send_half(spatial[0], 0)
+        halve(temporal[2], 1)
     for n, i in enumerate((2, 1, 0)):
         with jax.named_scope("c%d_w" % (n + 1)):
             finish_direct(s_shared[i])
@@ -591,11 +600,10 @@
             send_half(spatial[n + 1], 0)
         with jax.named_scope("c%d_halve" % (n + 1)):
             halve(spatial[n], 0)
-            if n == 1:
-                halve(temporal[3], 1)
+            if n < 2:
+                halve(temporal[3 - 3 * n], 1)
     with jax.named_scope("c4_halve"):
         halve(spatial[3], 0)
-        halve(temporal[0], 1)
     for step in range(1, bits - 1):
         with jax.named_scope("d%d_t" % step):
             add_bottles(step)
@@ -613,6 +621,10 @@
         with jax.named_scope("e2_s%d" % n):
             settle(it)
     with jax.named_scope("e3_drain"):
+        sent.append((t_mg.at[:, pl.ds(0, data_groups - 1)], d_sem.at[5]))
+        sent.append((s_mg.at[:, pl.ds(0, data_groups - 1)], d_sem.at[7]))
+        sent.append((part.at[:, pl.ds(0, frame_groups - 2)], rs_sem))
+        sent.append((final.at[:, pl.ds(0, 2 * column_groups - 1)], xs_sem))
         for view, sem in sent:
             drain(view, sem)
         for copy in bottle_copies:
@@ -719,10 +731,12 @@
             * 2,
             pltpu.SemaphoreType.DMA((10,)),
             pltpu.SemaphoreType.DMA((2, 4)),
-            pltpu.SemaphoreType.DMA((3, 12)),
+            pltpu.SemaphoreType.DMA((8,)),
+            pltpu.SemaphoreType.DMA((15,)),
             pltpu.SemaphoreType.DMA((8, bits - 1)),
+            pltpu.SemaphoreType.DMA,
             pltpu.SemaphoreType.DMA((8,)),
-            pltpu.SemaphoreType.DMA((2, 8)),
+            pltpu.SemaphoreType.DMA,
             pltpu.SemaphoreType.DMA((2, bits)),
         ],
         compiler_params=pltpu.CompilerParams(

time: 47.3 us -> 47 us (level)
  no operation moved by 1% of the time
where the time goes in v5:
time: 47 us; the launch traced here: 46.9 us
  Pallas kernels  46.2 us (98%)
  between operations  0.64 us (1%)
    pallas_call x1, Pallas kernels, per_device(): pl.pallas_call(functools.partial(kernel, frame_groups, row_groups, column...  45.4 us

profile of v5, /device:TPU:0, one launch (start us, length us, event | category | flops | bytes accessed | tf_op | source)
XLA Modules:
  0.0 46.9 jit_solution(1687386146983105058)
XLA Ops:
  0.6 45.4 %shard_map.127 = (bf16[64,1024]{1,0:T(8,128)(2,1)S(1)}, bf16[4,1024]{1,0:T(4,128)(2,1)S(1)}, bf16[32,1536]{1,0:T(8,128)(2,1)S(1)}, bf16[32,512]{1,0:T(8,128)(2,1...) custom-call(bf16[64,1024]{1,0:T(8,128)(2,1)} %bitcast.6, bf16[4,1024]{1,0:T(4,128)(2,1)} %bitcast.8, ...), custom_call_target="tpu_custom_call" | custom-call | tf_op jit(solution)/shard_map/pallas_call | solution.py:695
  46.1 0.8 %shard_map.128 = (bf16[64,1024]{1,0:T(8,128)(2,1)}, bf16[4,1024]{1,0:T(4,128)(2,1)}, bf16[32,1536]{1,0:T(8,128)(2,1)}, bf16[32,512]{1,0:T(8,128)(2,1)}, bf16[32,...) custom-call(bf16[64,1024]{1,0:T(8,128)(2,1)S(1)} %get-tuple-element.18.refs_0_, bf16[4,1024]{1,0:T(4,128)(2,1)S(1)} %get-tuple-element.19.refs_1_, ...), custom_call_target="tpu_custom_call" | custom-call | tf_op jit(solution)/shard_map/pallas_call | solution.py:760

commit v6 on v5

--- a/solution.py
+++ b/solution.py
@@ -10,6 +10,7 @@
 
 HEADS = 8
 LANES = 128
+PIECES = (4, 5, 6, 7)
 EPSILON = 1e-05
 MESH = pl.DeviceIdType.MESH
 F32 = jnp.float32
@@ -186,6 +187,7 @@
         dr_sem,
         r_sem,
         rs_sem,
+        p_sem,
         x_sem,
         xs_sem,
         b_sem,
@@ -374,45 +376,68 @@
         first, count, index = item
         half = frame_groups >> (step + 1)
         slots = pl.ds(first, count)
+        away = pl.ds((1 - side[step]) * half, half)
+        if step == bits - 2 and index in PIECES:
+            for k in reversed(range(column_groups)):
+                column = lax.rem(column_at + k, column_groups)
+                push(
+                    sums[step].at[slots, away, column],
+                    received[step].at[slots, :, column],
+                    rs_sem,
+                    p_sem.at[PIECES.index(index), k],
+                    {"frame": across(1 << step)},
+                )
+            return
         push(
-            sums[step].at[slots, pl.ds((1 - side[step]) * half, half)],
+            sums[step].at[slots, away],
             received[step].at[slots],
             rs_sem,
             r_sem.at[index, step],
             {"frame": across(1 << step)},
         )
 
-    def send_owners(item):
+    def send_owner(item, k):
         first, count, index = item
         step = bits - 1
         slots = pl.ds(first, count)
-        for k in reversed(range(column_groups)):
-            owner = lax.rem(column_at + k, column_groups)
-            for far in (1, 0) if k else (1,):
-                frame_to = across(1 << step) if far else frame
-                choice = 1 - side[step] if far else side[step]
-                push(
-                    sums[step].at[slots, choice, owner],
-                    final.at[slots, far * column_groups + column_at],
-                    xs_sem,
-                    x_sem.at[index],
-                    {"dp": clip(row_at, owner), "frame": frame_to},
-                )
-        for slot in range(first, first + count):
-            final[slot, column_at] = sums[step][slot, side[step], column_at]
+        owner = lax.rem(column_at + k, column_groups)
+        for far in (1, 0) if k else (1,):
+            push(
+                sums[step].at[slots, 1 - side[step] if far else side[step], owner],
+                final.at[slots, far * column_groups + column_at],
+                xs_sem,
+                x_sem.at[index],
+                {"dp": clip(row_at, owner), "frame": across(1 << step) if far else frame},
+            )
+        if not k:
+            for slot in range(first, first + count):
+                final[slot, column_at] = sums[step][slot, side[step], column_at]
 
     def halve(item, step):
         first, count, index = item
         half = frame_groups >> (step + 1)
+        near = pl.ds(side[step] * half, half)
+        if step == bits - 2 and index in PIECES:
+            for k in reversed(range(column_groups)):
+                column = lax.rem(column_at + k, column_groups)
+                view = received[step].at[pl.ds(first, count), :, column]
+                drain(view, p_sem.at[PIECES.index(index), k])
+                for slot in range(first, first + count):
+                    kept = sums[step][slot, near, column].astype(F32)
+                    total = kept + received[step][slot, :, column].astype(F32)
+                    sums[step + 1][slot, :, column] = total.astype(BF16)
+                send_owner(item, k)
+            return
         drain(received[step].at[pl.ds(first, count)], r_sem.at[index, step])
         for slot in range(first, first + count):
-            kept = sums[step][slot, pl.ds(side[step] * half, half)].astype(F32)
+            kept = sums[step][slot, near].astype(F32)
             total = kept + received[step][slot].astype(F32)
             sums[step + 1][slot] = total.astype(BF16)
         if step < bits - 2:
             send_half(item, step + 1)
             return
-        send_owners(item)
+        for k in reversed(range(column_groups)):
+            send_owner(item, k)
 
     def settle(item):
         first, count, index = item
@@ -454,17 +479,18 @@
 
 
     attended, s_saved = attend(s_low, se_ref, real_rows, enter)
+    with jax.named_scope("a02_enter"):
+        loads["og"].wait()
+        pl.semaphore_wait(barrier, frame_groups + data_groups - 2)
+        t_c_shared = share(t_c_send, t_c, flat(og_send, patches), True, 4)
+        s_nl_shared = share(s_nl_send, s_nl, s_low, True, 0)
     with jax.named_scope("a02_states"):
         loads["so"].wait()
         states = (tokens[:patches] + dot(attended[:patches], so_ref[...], 1, 1)).astype(BF16)
         st_send[...] = states.astype(F32).reshape(frame_groups, group, model).astype(BF16)
-        pl.semaphore_wait(barrier, frame_groups + data_groups - 2)
     with jax.named_scope("a03_enter"):
         exchange_frames(st_send, st_recv, 0)
-        loads["og"].wait()
         exchange_frames(og_send, og_recv, 1, far_first=False)
-        t_c_shared = share(t_c_send, t_c, flat(og_send, patches), True, 4)
-        s_nl_shared = share(s_nl_send, s_nl, s_low, True, 0)
         s_att_shared = share(s_att_send, s_att, attended, False, 1)
 
     t_rows = frame_groups * group
@@ -474,6 +500,7 @@
         turned_se[...] = se_ref[...].T
     with jax.named_scope("a04_relays"):
         relay(t_c_shared)
+        relay(s_nl_shared)
     def same_patch(shape):
         row_patch = lax.broadcasted_iota(jnp.int32, shape, 0) & (group - 1)
         column_patch = lax.broadcasted_iota(jnp.int32, shape, 1) & (group - 1)
@@ -506,7 +533,6 @@
         exchange_frames(sg_send, sg_recv, 2)
 
     with jax.named_scope("a08_relays"):
-        relay(s_nl_shared)
         relay(s_att_shared)
         arrive_frames(at_recv, 3)
         t_att_shared = share_direct(t_att_send, t_att, flat(at_recv, patches), False, 3)
@@ -735,6 +761,7 @@
             pltpu.SemaphoreType.DMA((15,)),
             pltpu.SemaphoreType.DMA((8, bits - 1)),
             pltpu.SemaphoreType.DMA,
+            pltpu.SemaphoreType.DMA((len(PIECES), column_groups)),
             pltpu.SemaphoreType.DMA((8,)),
             pltpu.SemaphoreType.DMA,
             pltpu.SemaphoreType.DMA((2, bits)),

time: 47 us -> 46.6 us (level)
  no operation moved by 1% of the time
where the time goes in v6:
time: 46.6 us; the launch traced here: 46.4 us
  Pallas kernels  45.8 us (98%)
  between operations  0.64 us (1%)
    pallas_call x1, Pallas kernels, per_device(): pl.pallas_call(functools.partial(kernel, frame_groups, row_groups, column...  45 us

profile of v6, /device:TPU:0, one launch (start us, length us, event | category | flops | bytes accessed | tf_op | source)
XLA Modules:
  0.0 46.4 jit_solution(2713070320203222514)
XLA Ops:
  0.6 45.0 %shard_map.127 = (bf16[64,1024]{1,0:T(8,128)(2,1)S(1)}, bf16[4,1024]{1,0:T(4,128)(2,1)S(1)}, bf16[32,1536]{1,0:T(8,128)(2,1)S(1)}, bf16[32,512]{1,0:T(8,128)(2,1...) custom-call(bf16[64,1024]{1,0:T(8,128)(2,1)} %bitcast.6, bf16[4,1024]{1,0:T(4,128)(2,1)} %bitcast.8, ...), custom_call_target="tpu_custom_call" | custom-call | tf_op jit(solution)/shard_map/pallas_call | solution.py:721
  45.6 0.8 %shard_map.128 = (bf16[64,1024]{1,0:T(8,128)(2,1)}, bf16[4,1024]{1,0:T(4,128)(2,1)}, bf16[32,1536]{1,0:T(8,128)(2,1)}, bf16[32,512]{1,0:T(8,128)(2,1)}, bf16[32,...) custom-call(bf16[64,1024]{1,0:T(8,128)(2,1)S(1)} %get-tuple-element.18.refs_0_, bf16[4,1024]{1,0:T(4,128)(2,1)S(1)} %get-tuple-element.19.refs_1_, ...), custom_call_target="tpu_custom_call" | custom-call | tf_op jit(solution)/shard_map/pallas_call | solution.py:787

commit v7 on v6

--- a/solution.py
+++ b/solution.py
@@ -10,7 +10,7 @@
 
 HEADS = 8
 LANES = 128
-PIECES = (4, 5, 6, 7)
+PIECES = (5, 6, 7)
 EPSILON = 1e-05
 MESH = pl.DeviceIdType.MESH
 F32 = jnp.float32
@@ -255,9 +255,10 @@
                 peer = peer + (1 << s) * (1 - 2 * side[s])
         return peer
 
-    def exchange_frames(send, dst, phase, far_first=True):
-        order = range(1, frame_groups)
-        for k in reversed(order) if far_first else order:
+    near = list(range(1, frame_groups))
+
+    def exchange_frames(send, dst, phase, order):
+        for k in order:
             peer = across(k)
             push(
                 send.at[peer],
@@ -489,8 +490,8 @@
         states = (tokens[:patches] + dot(attended[:patches], so_ref[...], 1, 1)).astype(BF16)
         st_send[...] = states.astype(F32).reshape(frame_groups, group, model).astype(BF16)
     with jax.named_scope("a03_enter"):
-        exchange_frames(st_send, st_recv, 0)
-        exchange_frames(og_send, og_recv, 1, far_first=False)
+        exchange_frames(st_send, st_recv, 0, near[::-1])
+        exchange_frames(og_send, og_recv, 1, near)
         s_att_shared = share(s_att_send, s_att, attended, False, 1)
 
     t_rows = frame_groups * group
@@ -515,7 +516,7 @@
         t_nl_shared = share_direct(t_nl_send, t_nl, t_low, True, 2)
         attended, t_saved = attend(t_low, te_ref, same_patch)
         at_send[...] = attended.astype(F32).reshape(at_send.shape).astype(BF16)
-        exchange_frames(at_send, at_recv, 3)
+        exchange_frames(at_send, at_recv, 3, near)
     with jax.named_scope("a06_waitog"):
         arrive_frames(og_recv, 1)
     t_cot = og_recv[...].astype(F32).reshape(t_rows, model)
@@ -530,7 +531,7 @@
         mixture_grad = backward_mixture(t_cot_low, to_ref, t_saved, keep_temporal)
         state_grads = backward_inputs(mixture_grad, turned_te, t_cot, t_normed[...], t_inverse)
         sg_send[...] = state_grads.reshape(frame_groups, group, model).astype(BF16)
-        exchange_frames(sg_send, sg_recv, 2)
+        exchange_frames(sg_send, sg_recv, 2, near[::-1])
 
     with jax.named_scope("a08_relays"):
         relay(s_att_shared)
@@ -628,6 +629,8 @@
             halve(spatial[n], 0)
             if n < 2:
                 halve(temporal[3 - 3 * n], 1)
+            else:
+                halve(spatial[0], 1)
     with jax.named_scope("c4_halve"):
         halve(spatial[3], 0)
     for step in range(1, bits - 1):
@@ -638,7 +641,8 @@
                     halve(it, step)
         for n, it in enumerate(spatial):
             with jax.named_scope("d%d_s%d" % (step, n)):
-                halve(it, step)
+                if n or step > 1:
+                    halve(it, step)
     with jax.named_scope("e1_t"):
         add_bottles(bits - 1)
         for it in temporal[1:] + temporal[:1]:

time: 46.6 us -> 46.2 us (level)
  no operation moved by 1% of the time
where the time goes in v7:
time: 46.2 us; the launch traced here: 46 us
  Pallas kernels  45.4 us (98%)
  between operations  0.64 us (1%)
    pallas_call x1, Pallas kernels, per_device(): pl.pallas_call(functools.partial(kernel, frame_groups, row_groups, column...  44.6 us

profile of v7, /device:TPU:0, one launch (start us, length us, event | category | flops | bytes accessed | tf_op | source)
XLA Modules:
  0.0 46.0 jit_solution(10777077204034139056)
XLA Ops:
  0.6 44.6 %shard_map.127 = (bf16[64,1024]{1,0:T(8,128)(2,1)S(1)}, bf16[4,1024]{1,0:T(4,128)(2,1)S(1)}, bf16[32,1536]{1,0:T(8,128)(2,1)S(1)}, bf16[32,512]{1,0:T(8,128)(2,1...) custom-call(bf16[64,1024]{1,0:T(8,128)(2,1)} %bitcast.6, bf16[4,1024]{1,0:T(4,128)(2,1)} %bitcast.8, ...), custom_call_target="tpu_custom_call" | custom-call | tf_op jit(solution)/shard_map/pallas_call | solution.py:725
  45.3 0.8 %shard_map.128 = (bf16[64,1024]{1,0:T(8,128)(2,1)}, bf16[4,1024]{1,0:T(4,128)(2,1)}, bf16[32,1536]{1,0:T(8,128)(2,1)}, bf16[32,512]{1,0:T(8,128)(2,1)}, bf16[32,...) custom-call(bf16[64,1024]{1,0:T(8,128)(2,1)S(1)} %get-tuple-element.18.refs_0_, bf16[4,1024]{1,0:T(4,128)(2,1)S(1)} %get-tuple-element.19.refs_1_, ...), custom_call_target="tpu_custom_call" | custom-call | tf_op jit(solution)/shard_map/pallas_call | solution.py:791

commit v8 on v7

--- a/solution.py
+++ b/solution.py
@@ -10,7 +10,7 @@
 
 HEADS = 8
 LANES = 128
-PIECES = (5, 6, 7)
+PIECES = (6, 7)
 EPSILON = 1e-05
 MESH = pl.DeviceIdType.MESH
 F32 = jnp.float32

time: 46.2 us -> 46.2 us (level)
  no operation moved by 1% of the time
where the time goes in v8:
time: 46.2 us; the launch traced here: 46 us
  Pallas kernels  45.4 us (98%)
  between operations  0.64 us (1%)
    pallas_call x1, Pallas kernels, per_device(): pl.pallas_call(functools.partial(kernel, frame_groups, row_groups, column...  44.6 us

profile of v8, /device:TPU:0, one launch (start us, length us, event | category | flops | bytes accessed | tf_op | source)
XLA Modules:
  0.0 46.0 jit_solution(16936602453829714777)
XLA Ops:
  0.6 44.6 %shard_map.127 = (bf16[64,1024]{1,0:T(8,128)(2,1)S(1)}, bf16[4,1024]{1,0:T(4,128)(2,1)S(1)}, bf16[32,1536]{1,0:T(8,128)(2,1)S(1)}, bf16[32,512]{1,0:T(8,128)(2,1...) custom-call(bf16[64,1024]{1,0:T(8,128)(2,1)} %bitcast.6, bf16[4,1024]{1,0:T(4,128)(2,1)} %bitcast.8, ...), custom_call_target="tpu_custom_call" | custom-call | tf_op jit(solution)/shard_map/pallas_call | solution.py:725
  45.2 0.8 %shard_map.128 = (bf16[64,1024]{1,0:T(8,128)(2,1)}, bf16[4,1024]{1,0:T(4,128)(2,1)}, bf16[32,1536]{1,0:T(8,128)(2,1)}, bf16[32,512]{1,0:T(8,128)(2,1)}, bf16[32,...) custom-call(bf16[64,1024]{1,0:T(8,128)(2,1)S(1)} %get-tuple-element.18.refs_0_, bf16[4,1024]{1,0:T(4,128)(2,1)S(1)} %get-tuple-element.19.refs_1_, ...), custom_call_target="tpu_custom_call" | custom-call | tf_op jit(solution)/shard_map/pallas_call | solution.py:791
